TPU v7x, 32 devices: a whole 2x2x4 slice. The times are simulated.
32 devices in a mesh: dp: 2 (over x), tp: 4 (over z), sp: 4 (over y, core).
Axes of the slice: x: 2, y: 2, z: 4, core: 2. Of those that a mesh axis runs over, the one named last changes fastest.
Arguments:
- x: bfloat16 [4096, 4096], P(('dp', 'sp')), parts along dimension 0
- pos: int32 [4096], P(('dp', 'sp')), parts along dimension 0
- k_hist: bfloat16 [2, 16384, 8, 128], P(None, ('dp', 'sp'), 'tp'), parts along dimension 1
- v_hist: bfloat16 [2, 16384, 8, 128], P(None, ('dp', 'sp'), 'tp'), parts along dimension 1
- wq: bfloat16 [2, 4096, 4096], P(None, None, 'tp')
- wk: bfloat16 [2, 4096, 1024], P(None, None, 'tp')
- wv: bfloat16 [2, 4096, 1024], P(None, None, 'tp')
- wo: bfloat16 [2, 4096, 4096], P(None, 'tp')
- wg: bfloat16 [2, 4096, 14336], P(None, None, 'tp')
- wu: bfloat16 [2, 4096, 14336], P(None, None, 'tp')
- wd: bfloat16 [2, 14336, 4096], P(None, 'tp')
- g1: bfloat16 [2, 4096], replicated
- g2: bfloat16 [2, 4096], replicated
Outputs:
- output 1: bfloat16 [4096, 4096], P(('dp', 'sp')), parts along dimension 0
- output 2: bfloat16 [2, 4096, 8, 128], P(None, ('dp', 'sp'), 'tp'), parts along dimension 1
- output 3: bfloat16 [2, 4096, 8, 128], P(None, ('dp', 'sp'), 'tp'), parts along dimension 1
There are 2 independent parts. A program takes and returns all parts, laid end to end along the dimension named above; an argument that names none is the same for every part.
All inputs are finite; a program needn't handle non-finite values.
Results may differ from a plain program's by a relative error of at most 0.02.
Values are sent between devices in bfloat16 or wider.
A program may use at most 1 GiB of HBM per device.

v0:
```python
import jax
import jax.numpy as jnp
from jax import lax
from jax.sharding import PartitionSpec as P

EPS = 1e-5
ROPE_THETA = 500000.0
QB = 64


def rmsnorm(x, g):
    xf = x.astype(jnp.float32)
    r = lax.rsqrt(jnp.mean(xf * xf, axis=-1, keepdims=True) + EPS)
    return (xf * r * g.astype(jnp.float32)).astype(jnp.bfloat16)


def rope(t, pos):
    half = t.shape[-1] // 2
    inv = ROPE_THETA ** (-(jnp.arange(half, dtype=jnp.float32) * (2.0 / t.shape[-1])))
    ang = pos.astype(jnp.float32)[..., None] * inv
    c = jnp.cos(ang)[..., None, :]
    s = jnp.sin(ang)[..., None, :]
    tf = t.astype(jnp.float32)
    t1 = tf[..., :half]
    t2 = tf[..., half:]
    return jnp.concatenate([t1 * c - t2 * s, t2 * c + t1 * s], axis=-1).astype(jnp.bfloat16)


def mm(a, b):
    return jnp.dot(a, b, preferred_element_type=jnp.float32)


def partial_attn(qq, k, v, mask=None):
    s = jnp.einsum('qkgd,tkd->qkgt', qq, k, preferred_element_type=jnp.float32) * (k.shape[-1] ** -0.5)
    if mask is not None:
        s = jnp.where(mask, s, -jnp.inf)
    m = jnp.max(s, axis=-1)
    p = jnp.exp(s - m[..., None])
    o = jnp.einsum('qkgt,tkd->qkgd', p.astype(jnp.bfloat16), v, preferred_element_type=jnp.float32)
    return m, jnp.sum(p, axis=-1), o


def solution(mesh):
    sp = mesh.shape['sp']
    row = ('dp', 'sp')
    kv_spec = P(None, row, 'tp', None)
    col = P(None, None, 'tp')
    rowsplit = P(None, 'tp', None)

    def body(x, pos, k_hist, v_hist, wq, wk, wv, wo, wg, wu, wd, g1, g2):
        n, d = x.shape
        layers, _, kvl, dh = k_hist.shape
        hql = wq.shape[-1] // dh
        g = hql // kvl
        s_tot = n * sp
        idx = lax.axis_index('sp')
        kpos = jnp.arange(s_tot)
        starts = idx * n + jnp.arange(n // QB) * QB
        ks, vs = [], []
        for l in range(layers):
            h = rmsnorm(x, g1[l])
            q = rope(mm(h, wq[l]).astype(jnp.bfloat16).reshape(n, hql, dh), pos)
            k = rope(mm(h, wk[l]).astype(jnp.bfloat16).reshape(n, kvl, dh), pos)
            v = mm(h, wv[l]).astype(jnp.bfloat16).reshape(n, kvl, dh)
            ks.append(k)
            vs.append(v)

            q_all = lax.all_gather(q, 'sp', axis=0, tiled=True).reshape(s_tot // QB, QB, kvl, g, dh)
            kh = k_hist[l]
            vh = v_hist[l]
            m_h, l_h, o_h = lax.map(lambda qq: partial_attn(qq, kh, vh), q_all)
            m_h = m_h.reshape(s_tot, kvl, g)
            m_g = lax.pmax(m_h, 'sp')
            sc = jnp.exp(m_h - m_g)
            o_h = lax.psum_scatter(o_h.reshape(s_tot, kvl, g, dh) * sc[..., None], 'sp', scatter_dimension=0, tiled=True)
            l_h = lax.psum_scatter(l_h.reshape(s_tot, kvl, g) * sc, 'sp', scatter_dimension=0, tiled=True)
            m_h = lax.dynamic_slice_in_dim(m_g, idx * n, n, axis=0)

            k_all = lax.all_gather(k, 'sp', axis=0, tiled=True)
            v_all = lax.all_gather(v, 'sp', axis=0, tiled=True)

            def new_blk(args, k_all=k_all, v_all=v_all):
                st, qq = args
                mask = (kpos[None, :] <= (st + jnp.arange(QB))[:, None])[:, None, None, :]
                return partial_attn(qq, k_all, v_all, mask)

            m_n, l_n, o_n = lax.map(new_blk, (starts, q.reshape(n // QB, QB, kvl, g, dh)))
            m_n = m_n.reshape(n, kvl, g)
            l_n = l_n.reshape(n, kvl, g)
            o_n = o_n.reshape(n, kvl, g, dh)
            mt = jnp.maximum(m_h, m_n)
            a_h = jnp.exp(m_h - mt)
            a_n = jnp.exp(m_n - mt)
            den = l_h * a_h + l_n * a_n
            o = (o_h * a_h[..., None] + o_n * a_n[..., None]) / den[..., None]
            attn = o.astype(jnp.bfloat16).reshape(n, hql * dh)
            x = x + lax.psum(mm(attn, wo[l]), 'tp').astype(jnp.bfloat16)

            h2 = rmsnorm(x, g2[l])
            a = mm(h2, wg[l]).astype(jnp.bfloat16)
            b = mm(h2, wu[l]).astype(jnp.bfloat16)
            u = (jax.nn.silu(a.astype(jnp.float32)) * b.astype(jnp.float32)).astype(jnp.bfloat16)
            x = x + lax.psum(mm(u, wd[l]), 'tp').astype(jnp.bfloat16)
        return x, jnp.stack(ks), jnp.stack(vs)

    in_specs = (P(row, None), P(row), kv_spec, kv_spec, col, col, col, rowsplit, col, col, rowsplit, P(), P())
    out_specs = (P(row, None), kv_spec, kv_spec)
    return jax.shard_map(body, mesh=mesh, in_specs=in_specs, out_specs=out_specs, check_vma=False)
```

profile of v0, /device:TPU:0, one launch (start us, length us, event | category | flops | bytes accessed | tf_op | source)
XLA Modules:
  0.0 2168.9 jit_solution(10276330387345192833)
XLA Ops:
  8.8 3.1 fusion.102
  11.9 7.0 convert_bitcast_fusion.1
  24.8 4.4 fusion.194
  31.1 3.6 fusion.224
  34.6 2.2 fusion.225
  37.1 24.7 %all-gather.7.cloned.1.call-done = bf16[2048,8,128]{2,0,1:T(8,128)(2,1)} async-done(((bf16[512,8,128]{2,0,1:T(8,128)(2,1)}), bf16[2048,8,128]{2,0,1:T(8,128)(2,1)}) %all-gather.7.cloned.1.call-update) | async-done | bytes 4194320 | tf_op jit(solution)/shard_map/all_gather | solution.py:68
  61.8 4.3 broadcast.187.clone2
  66.8 182.3 %while.58 = (s32[]{:T(128)}, f32[32,64,2,4]{1,0,3,2:T(8,128)S(1)}, f32[32,64,2,4]{1,0,3,2:T(8,128)}, f32[32,64,2,4,128]{4,1,0,3,2:T(8,128)}, bf16[32,64,2,4,128]...) while((s32[]{:T(128)}, f32[32,64,2,4]{1,0,3,2:T(8,128)S(1)}, ...), condition=%wide.region_4.5_spmd, body=%wide.region_1.4_spmd.sunk | while | flops 545258496 | bytes 15090789 | solution.py:71
  250.0 2.4 pad_maximum_fusion.5
  252.4 4.5 fusion.197
  258.0 23.6 %all-reduce.7.cloned.1.call-done = f32[2048,2,4]{0,2,1:T(4,128)} async-done(((f32[2048,2,4]{0,2,1:T(4,128)}), f32[2048,2,4]{0,2,1:T(4,128)}) %all-reduce.7.cloned.1.call-update) | async-done | bytes 65552 | tf_op jit(solution)/shard_map/pmax | solution.py:73
  283.9 8.0 bitcast_multiply_fusion.1
  296.1 2.0 pad_maximum_fusion
  298.1 2.3 copy.120
  302.3 16.9 all-gather.11.cloned.1.call-done
  319.5 45.2 %while.60 = (s32[]{:T(128)}, f32[8,64,2,4]{1,0,3,2:T(8,128)S(1)}, f32[8,64,2,4]{1,0,3,2:T(8,128)S(1)}, f32[8,64,2,4,128]{4,1,0,3,2:T(8,128)S(1)}, s32[8]{0:T(128...) while((s32[]{:T(128)}, f32[8,64,2,4]{1,0,3,2:T(8,128)S(1)}, ...), condition=%wide.region_10.11_spmd.clone, body=%wide.region_7.10_spmd.clone.sunk | while | flops 548535360 | bytes 19811484 | solution.py:87
  320.9 1.8 bitcast_reduce_fusion.10
  326.5 1.8 bitcast_reduce_fusion.10
  332.2 1.8 bitcast_reduce_fusion.10
  360.4 1.8 bitcast_reduce_fusion.10
  367.1 53.2 %reduce-scatter.9.cloned.1.call-done = f32[512,2,4,128]{3,0,2,1:T(8,128)} async-done(((f32[2048,2,4,128]{3,0,2,1:T(8,128)}), f32[512,2,4,128]{3,0,2,1:T(8,128)}) %reduce-scatter.9.cloned.1.call-update) | async-done | bytes 2097168 | tf_op jit(solution)/shard_map/reduce_scatter | solution.py:75
  420.3 4.5 fusion.169
  426.3 10.2 fusion.118
  436.5 287.7 %all-reduce.10 = bf16[512,4096]{1,0:T(8,128)(2,1)} all-reduce(f32[512,4096]{1,0:T(8,128)} %fusion.118), channel_id=1, replica_groups=mesh['dp'=2,'tp'=4,'sp'=4] {'tp'}, use_global_device_ids=true, to_apply=%region_12.13 | all-reduce | flops 2097152 | bytes 12582912 | tf_op jit(solution)/shard_map/psum | solution.py:97
  724.2 7.4 fusion.105
  731.7 23.5 %fusion.136 = bf16[512,3584]{1,0:T(8,128)(2,1)} fusion(bf16[2,4096,3584]{2,1,0:T(8,128)(2,1)} %param.29, bf16[512,4096]{1,0:T(8,128)(2,1)} %get-tuple-element.403, f32[4096]{0:T(1024)S(1)} %bitcast.506, f32[512]{0:T(512)S(1)} %add_rsqrt_fusion.2), kind=kOutput, calls=%fused_computation.142 | convolution fusion | flops 15042609152 | bytes 37242880 | tf_op jit(solution)/shard_map/dot_general | solution.py:30
  755.2 24.2 %fusion.262 = bf16[512,3584]{1,0:T(8,128)(2,1)} fusion(bf16[512,3584]{1,0:T(8,128)(2,1)} %fusion.136, bf16[2,4096,3584]{2,1,0:T(8,128)(2,1)} %param.30, bf16[512,4096]{1,0:T(8,128)(2,1)} %get-tuple-element.403, f32[4096]{0:T(1024)S(1)} %bitcast.507, f32[512]{0:T(512)S(1)} %add_rsqrt_fusion.2), kind=kOutput, calls=%fused_computation.141.clone.clone.2 | convolution fusion | flops 15057289216 | bytes 40912896 | tf_op jit(solution)/shard_map/dot_general | solution.py:30
  779.4 23.9 %fusion.90 = f32[512,4096]{1,0:T(8,128)} fusion(bf16[2,3584,4096]{2,1,0:T(8,128)(2,1)} %param.31, bf16[512,3584]{1,0:T(8,128)(2,1)} %fusion.262), kind=kOutput, calls=%fused_computation.82 | convolution fusion | flops 15032385536 | bytes 41418752 | tf_op jit(solution)/shard_map/dot_general | solution.py:30
  803.3 279.6 %all-reduce.11 = bf16[512,4096]{1,0:T(8,128)(2,1)} all-reduce(f32[512,4096]{1,0:T(8,128)} %fusion.90), channel_id=1, replica_groups=mesh['dp'=2,'tp'=4,'sp'=4] {'tp'}, use_global_device_ids=true, to_apply=%region_14.15 | all-reduce | flops 2097152 | bytes 12582912 | tf_op jit(solution)/shard_map/psum | solution.py:103
  1083.0 5.5 fusion.108
  1088.5 8.5 convert_bitcast_fusion
  1102.4 2.0 copy_bitcast_fusion
  1105.2 3.4 fusion.200
  1109.5 2.0 copy.202
  1111.4 1.9 copy.203
  1113.4 2.6 subtract_convert_fusion.2
  1116.0 18.5 all-gather.13.cloned.1.call-done
  1134.5 4.3 broadcast.187.clone
  1139.5 182.4 %while.59 = (s32[]{:T(128)}, f32[32,64,2,4]{1,0,3,2:T(8,128)S(1)}, f32[32,64,2,4]{1,0,3,2:T(8,128)}, f32[32,64,2,4,128]{4,1,0,3,2:T(8,128)}, bf16[32,64,2,4,128]...) while((s32[]{:T(128)}, f32[32,64,2,4]{1,0,3,2:T(8,128)S(1)}, ...), condition=%wide.region_19.20_spmd, body=%wide.region_16.19_spmd.sunk | while | flops 545258496 | bytes 15090789 | solution.py:71
  1322.7 2.4 pad_maximum_fusion.6
  1325.2 4.5 fusion.203
  1330.8 23.6 %all-reduce.9.cloned.1.call-done = f32[2048,2,4]{0,2,1:T(4,128)} async-done(((f32[2048,2,4]{0,2,1:T(4,128)}), f32[2048,2,4]{0,2,1:T(4,128)}) %all-reduce.9.cloned.1.call-update) | async-done | bytes 65552 | tf_op jit(solution)/shard_map/pmax | solution.py:73
  1356.8 8.0 bitcast_multiply_fusion
  1369.6 2.1 pad_maximum_fusion.1
  1371.7 2.3 copy.139
  1374.1 2.5 pad_maximum_fusion.4
  1376.7 2.2 maximum_maximum_fusion
  1380.3 10.5 all-gather.17.cloned.1.call-done
  1391.1 44.6 %while.61 = (s32[]{:T(128)}, f32[8,64,2,4]{1,0,3,2:T(8,128)S(1)}, f32[8,64,2,4]{1,0,3,2:T(8,128)S(1)}, f32[8,64,2,4,128]{4,1,0,3,2:T(8,128)S(1)}, s32[8]{0:T(128...) while((s32[]{:T(128)}, f32[8,64,2,4]{1,0,3,2:T(8,128)S(1)}, ...), condition=%wide.region_25.26_spmd.clone, body=%wide.region_22.25_spmd.clone.sunk | while | flops 548535360 | bytes 19811484 | solution.py:87
  1398.0 1.8 bitcast_reduce_fusion.11
  1409.1 1.8 bitcast_reduce_fusion.11
  1414.7 1.8 bitcast_reduce_fusion.11
  1425.8 1.8 bitcast_reduce_fusion.11
  1431.4 1.8 bitcast_reduce_fusion.11
  1438.1 53.8 %reduce-scatter.11.cloned.1.call-done = f32[512,2,4,128]{3,0,2,1:T(8,128)} async-done(((f32[2048,2,4,128]{3,0,2,1:T(8,128)}), f32[512,2,4,128]{3,0,2,1:T(8,128)}) %reduce-scatter.11.cloned.1.call-update) | async-done | bytes 2097168 | tf_op jit(solution)/shard_map/reduce_scatter | solution.py:75
  1491.9 4.6 fusion.162
  1498.0 10.2 fusion.114
  1508.2 287.8 %all-reduce.12 = bf16[512,4096]{1,0:T(8,128)(2,1)} all-reduce(f32[512,4096]{1,0:T(8,128)} %fusion.114), channel_id=1, replica_groups=mesh['dp'=2,'tp'=4,'sp'=4] {'tp'}, use_global_device_ids=true, to_apply=%region_27.28 | all-reduce | flops 2097152 | bytes 12582912 | tf_op jit(solution)/shard_map/psum | solution.py:97
  1796.0 7.4 fusion.111
  1803.4 23.3 %fusion.142 = bf16[512,3584]{1,0:T(8,128)(2,1)} fusion(bf16[2,4096,3584]{2,1,0:T(8,128)(2,1)} %param.29, bf16[512,4096]{1,0:T(8,128)(2,1)} %get-tuple-element.394, f32[4096]{0:T(1024)S(1)} %bitcast.501, f32[512]{0:T(512)S(1)} %add_rsqrt_fusion), kind=kOutput, calls=%fused_computation.144 | convolution fusion | flops 15042609152 | bytes 37242880 | tf_op jit(solution)/shard_map/dot_general | solution.py:30
  1826.8 24.0 %fusion.258 = bf16[512,3584]{1,0:T(8,128)(2,1)} fusion(bf16[512,3584]{1,0:T(8,128)(2,1)} %fusion.142, bf16[2,4096,3584]{2,1,0:T(8,128)(2,1)} %param.30, bf16[512,4096]{1,0:T(8,128)(2,1)} %get-tuple-element.394, f32[4096]{0:T(1024)S(1)} %bitcast.502, f32[512]{0:T(512)S(1)} %add_rsqrt_fusion), kind=kOutput, calls=%fused_computation.140.clone.clone.2 | convolution fusion | flops 15057289216 | bytes 40912896 | tf_op jit(solution)/shard_map/dot_general | solution.py:30
  1850.7 24.0 %fusion.84 = f32[512,4096]{1,0:T(8,128)} fusion(bf16[2,3584,4096]{2,1,0:T(8,128)(2,1)} %param.31, bf16[512,3584]{1,0:T(8,128)(2,1)} %fusion.258), kind=kOutput, calls=%fused_computation.76 | convolution fusion | flops 15032385536 | bytes 41418752 | tf_op jit(solution)/shard_map/dot_general | solution.py:30
  1874.7 279.6 %all-reduce.13 = bf16[512,4096]{1,0:T(8,128)(2,1)} all-reduce(f32[512,4096]{1,0:T(8,128)} %fusion.84), channel_id=1, replica_groups=mesh['dp'=2,'tp'=4,'sp'=4] {'tp'}, use_global_device_ids=true, to_apply=%region_29.30 | all-reduce | flops 2097152 | bytes 12582912 | tf_op jit(solution)/shard_map/psum | solution.py:103
  2154.3 7.2 add.210
  (629 shorter events, 483.1 us)
Async XLA Ops:
  7.2 54.7 %all-gather.7.cloned.1.call-start = ((), (), s32[]{:S(2)}) async-start(), calls=%async_computation.4 | async-start | bytes 5242880 | tf_op jit(solution)/shard_map/all_gather | solution.py:68
  7.2 4.6 copy-start
  8.8 16.0 copy-start.28
  19.4 0.7 copy-start.29
  21.1 8.7 copy-start.7
  21.1 8.7 copy-start.9
  21.9 1.0 copy-start.3
  24.5 257.1 %all-reduce.7.cloned.1.call-start = ((), (), s32[]{:S(2)}) async-start(), calls=%async_computation.5 | async-start | bytes 131072 | tf_op jit(solution)/shard_map/pmax | solution.py:73
  29.8 4.8 copy-start.16
  31.1 218.9 %copy-start.11 = (bf16[512,2,64]{2,1,0:T(2,128)(2,1)}, bf16[512,2,64]{2,1,0:T(2,128)(2,1)S(1)}, u32[]{:S(2)}) copy-start(bf16[512,2,64]{2,1,0:T(2,128)(2,1)S(1)} %get-tuple-element.431) | copy-start | bytes 393220
  249.9 51.0 %all-gather.9.cloned.1.call-start = ((), (), s32[]{:S(2)}) async-start(), calls=%async_computation.7 | async-start | bytes 1310720 | tf_op jit(solution)/shard_map/all_gather | solution.py:79
  252.4 5.5 copy-start.23
  252.4 29.2 %copy-start.21 = (f32[2048,2,4]{0,2,1:T(4,128)S(1)}, f32[2048,2,4]{0,2,1:T(4,128)}, u32[]{:S(2)}) copy-start(f32[2048,2,4]{0,2,1:T(4,128)} %reshape.295) | copy-start | bytes 196612
  252.4 66.8 %all-gather.11.cloned.1.call-start = ((), (), s32[]{:S(2)}) async-start(), calls=%async_computation.8 | async-start | bytes 1310720 | tf_op jit(solution)/shard_map/all_gather | solution.py:80
  256.9 35.0 %copy-start.17 = (bf16[512,256]{0,1:T(8,128)(2,1)}, bf16[512,256]{0,1:T(8,128)(2,1)S(1)}, u32[]{:S(2)}) copy-start(bf16[512,256]{0,1:T(8,128)(2,1)S(1)} %fusion.197) | copy-start | bytes 786436
  257.8 107.1 %reduce-scatter.13.cloned.1.call-start = ((), (), s32[]{:S(2)}) async-start(), calls=%async_computation.14 | async-start | bytes 1310720
  283.9 136.4 %reduce-scatter.9.cloned.1.call-start = ((), (), s32[]{:S(2)}) async-start(), calls=%async_computation.6 | async-start | bytes 10485760 | tf_op jit(solution)/shard_map/reduce_scatter | solution.py:75
  291.9 1.2 copy-start.4
  292.0 842.5 %all-gather.13.cloned.1.call-start = ((), (), s32[]{:S(2)}) async-start(), calls=%async_computation.9 | async-start | bytes 5242880 | tf_op jit(solution)/shard_map/all_gather | solution.py:68
  296.1 4.2 copy-start.25
  319.5 3.2 copy-start.30
  325.1 3.2 copy-start.30
  330.8 3.2 copy-start.30
  336.4 3.2 copy-start.30
  342.1 3.2 copy-start.30
  347.7 3.2 copy-start.30
  353.4 3.2 copy-start.30
  359.0 3.2 copy-start.30
  364.7 61.6 %copy-start.32 = (s32[8]{0:T(128)}, s32[8]{0:T(128)S(1)}, u32[]{:S(2)}) copy-start(s32[8]{0:T(128)S(1)} %get-tuple-element.813) | copy-start | bytes 100
  1083.0 5.5 copy-start.26
  1088.4 8.5 copy-start.1
  1097.5 1.0 copy-start.8
  1097.5 1.0 copy-start.10
  1099.3 1.0 copy-start.5
  1102.0 252.4 %all-reduce.9.cloned.1.call-start = ((), (), s32[]{:S(2)}) async-start(), calls=%async_computation.10 | async-start | bytes 131072 | tf_op jit(solution)/shard_map/pmax | solution.py:73
  1102.4 2.8 copy-start.2
  1139.5 183.2 %copy-start.14 = (bf16[512,2,64]{2,1,0:T(2,128)(2,1)S(1)}, bf16[512,2,64]{2,1,0:T(2,128)(2,1)}, u32[]{:S(2)}) copy-start(bf16[512,2,64]{2,1,0:T(2,128)(2,1)} %get-tuple-element.429) | copy-start | bytes 393220
  1322.7 56.2 %all-gather.15.cloned.1.call-start = ((), (), s32[]{:S(2)}) async-start(), calls=%async_computation.12 | async-start | bytes 1310720 | tf_op jit(solution)/shard_map/all_gather | solution.py:79
  1325.1 5.5 copy-start.24
  1325.1 29.2 %copy-start.22 = (f32[2048,2,4]{0,2,1:T(4,128)S(1)}, f32[2048,2,4]{0,2,1:T(4,128)}, u32[]{:S(2)}) copy-start(f32[2048,2,4]{0,2,1:T(4,128)} %reshape.304) | copy-start | bytes 196612
  1325.2 65.7 %all-gather.17.cloned.1.call-start = ((), (), s32[]{:S(2)}) async-start(), calls=%async_computation.13 | async-start | bytes 1310720 | tf_op jit(solution)/shard_map/all_gather | solution.py:80
  1329.7 35.2 %copy-start.19 = (bf16[512,256]{0,1:T(8,128)(2,1)}, bf16[512,256]{0,1:T(8,128)(2,1)S(1)}, u32[]{:S(2)}) copy-start(bf16[512,256]{0,1:T(8,128)(2,1)S(1)} %fusion.203) | copy-start | bytes 786436
  1330.6 105.2 %reduce-scatter.15.cloned.1.call-start = ((), (), s32[]{:S(2)}) async-start(), calls=%async_computation.15 | async-start | bytes 1310720
  1356.6 135.3 %reduce-scatter.11.cloned.1.call-start = ((), (), s32[]{:S(2)}) async-start(), calls=%async_computation.11 | async-start | bytes 10485760 | tf_op jit(solution)/shard_map/reduce_scatter | solution.py:75
  1364.9 1.0 copy-start.18
  1364.9 1.8 copy-start.6
  1369.6 4.4 copy-start.20
  1369.6 7.1 copy-start.12
  1369.6 7.1 copy-start.13
  1369.6 7.1 copy-start.15
  1374.0 17.1 copy-start.33
  1391.1 3.1 copy-start.31
  1396.7 3.1 copy-start.31
  1402.2 3.1 copy-start.31
  1407.8 3.1 copy-start.31
  1413.3 3.1 copy-start.31
  1418.9 3.1 copy-start.31
  1424.5 3.1 copy-start.31
  1430.0 3.2 copy-start.31
  1796.0 7.4 copy-start.27
Sparse Core Ops, SparseCore 0:
  24.6 37.1 all-gather.6
  250.0 31.5 all-reduce.6
  283.7 16.6 all-gather.8
  302.5 16.6 all-gather.10
  321.6 24.8 reduce-scatter.12
  348.9 71.3 reduce-scatter.8
  1102.1 32.3 all-gather.12
  1322.8 31.5 all-reduce.8
  1355.9 16.6 all-gather.14
  1374.1 16.6 all-gather.16
  1393.3 24.7 reduce-scatter.14
  1420.6 71.2 reduce-scatter.10
where the time goes:
time: 2180 us; the launch traced here: 2170 us
  blocking collectives  1130 us (52%)
  matrix products  463 us (21%)
  waiting for transfers between devices  225 us (10%)
  other arithmetic  168 us (8%)
  local copies, waits for them, and re-layouts  159 us (7%)
    psum x2, blocking collectives, body(): x = x + lax.psum(mm(attn, wo[l]), 'tp').astype(jnp.bfloat16)  575 us
    psum x2, blocking collectives, body(): x = x + lax.psum(mm(u, wd[l]), 'tp').astype(jnp.bfloat16)  559 us
    dot_general x14, matrix products, mm(): return jnp.dot(a, b, preferred_element_type=jnp.float32)  196 us
    dot_general x80, matrix products, partial_attn(): jnp.einsum('qkgd,tkd->qkgt', qq, k, preferred_element_type=jnp.float32)  137 us
    dot_general x80, matrix products, partial_attn(): jnp.einsum('qkgt,tkd->qkgd', p.astype(jnp.bfloat16), v, preferred_element...  130 us
    reduce_scatter x2, waiting for transfers between devices, body(): lax.psum_scatter(o_h.reshape(s_tot, kvl, g, dh) * sc[..., None], 'sp', sc...  107 us
    dynamic_update_slice x128, local copies, waits for them, and re-layouts, body(): m_h, l_h, o_h = lax.map(lambda qq: partial_attn(qq, kh, vh), q_all)  91.2 us
    reduce_sum x80, other arithmetic, partial_attn(): return (m, jnp.sum(p, axis=-1), o)  71.1 us
  transfers between devices with their start and end apart: 12, of which 8 were waited for; matrix products, arithmetic and copies ran while one was open for 8% of the time, Pallas kernels for 0%

commit v1 on v0

v1 whole, which is shorter than its diff:
```python
import functools

import jax
import jax.numpy as jnp
from jax import lax
from jax.experimental import pallas as pl
from jax.experimental.pallas import tpu as pltpu
from jax.sharding import PartitionSpec as P


EPS = 1e-5
ROPE_THETA = 500000.0
MESH = pl.DeviceIdType.MESH
LOG2E = 1.4426950408889634


def rope_tables(pos, dh):
    half = dh // 2
    inv = ROPE_THETA ** (-(jnp.arange(half, dtype=jnp.float32) * (2.0 / dh)))
    ang = pos.astype(jnp.float32)[:, None] * inv
    c, s = jnp.cos(ang), jnp.sin(ang)
    return jnp.concatenate([c, c], -1), jnp.concatenate([-s, s], -1)


def norm_into(x_ref, g_ref, h_ref):
    rb = 64
    for lo in range(0, x_ref.shape[0], rb):
        xf = x_ref[lo:lo + rb, :].astype(jnp.float32)
        r = lax.rsqrt(jnp.mean(xf * xf, axis=-1, keepdims=True) + EPS)
        h_ref[lo:lo + rb, :] = (xf * r * g_ref[...].astype(jnp.float32)).astype(jnp.bfloat16)


def qkv_kernel(nq, dh, x_ref, g_ref, c_ref, s_ref, wq_ref, wk_ref, wv_ref, q_ref, k_ref, v_ref, h_ref):
    i = pl.program_id(0)

    @pl.when(i == 0)
    def _():
        norm_into(x_ref, g_ref, h_ref)

    def rotated(w_ref, out):
        t = jnp.dot(h_ref[...], w_ref[...], preferred_element_type=jnp.float32)
        t = t.astype(jnp.bfloat16).astype(jnp.float32)
        for j in range(t.shape[1] // dh):
            th = t[:, j * dh:(j + 1) * dh]
            r = th * c_ref[...] + pltpu.roll(th, dh // 2, 1) * s_ref[...]
            out[:, j * dh:(j + 1) * dh] = r.astype(jnp.bfloat16)

    @pl.when(i < nq)
    def _():
        rotated(wq_ref, q_ref)

    @pl.when(i == nq)
    def _():
        rotated(wk_ref, k_ref)

    @pl.when(i == nq + 1)
    def _():
        v_ref[...] = jnp.dot(h_ref[...], wv_ref[...], preferred_element_type=jnp.float32).astype(jnp.bfloat16)


def qkv(x, g, c, s, wq, wk, wv, layer, dh):
    n, d = x.shape
    hq, hk = wq.shape[2], wk.shape[2]
    nc = 256
    nq = hq // nc
    vm = pl.BlockSpec(memory_space=pltpu.VMEM)
    bf = jnp.bfloat16
    return pl.pallas_call(
        functools.partial(qkv_kernel, nq, dh), grid=(nq + 2,),
        in_specs=[vm, vm, vm, vm,
                  pl.BlockSpec((None, d, nc), lambda i: (layer, 0, jnp.minimum(i, nq - 1))),
                  pl.BlockSpec((None, d, hk), lambda i: (layer, 0, 0)),
                  pl.BlockSpec((None, d, hk), lambda i: (layer, 0, 0))],
        out_specs=[pl.BlockSpec((n, nc), lambda i: (0, jnp.minimum(i, nq - 1))), vm, vm],
        out_shape=[jax.ShapeDtypeStruct((n, hq), bf), jax.ShapeDtypeStruct((n, hk), bf),
                   jax.ShapeDtypeStruct((n, hk), bf)],
        scratch_shapes=[pltpu.VMEM((n, d), bf)],
        cost_estimate=pl.CostEstimate(flops=2 * n * d * (hq + 2 * hk), bytes_accessed=2 * d * hq, transcendentals=0),
        compiler_params=pltpu.CompilerParams(vmem_limit_bytes=48 * 1024 * 1024),
        name="qkv",
    )(x, g, c, s, wq, wk, wv)


def gate_kernel(x_ref, g_ref, wg_ref, wu_ref, u_ref, h_ref):
    @pl.when(pl.program_id(0) == 0)
    def _():
        norm_into(x_ref, g_ref, h_ref)

    a = jnp.dot(h_ref[...], wg_ref[...], preferred_element_type=jnp.float32)
    b = jnp.dot(h_ref[...], wu_ref[...], preferred_element_type=jnp.float32)
    a = a.astype(jnp.bfloat16).astype(jnp.float32)
    b = b.astype(jnp.bfloat16).astype(jnp.float32)
    u_ref[...] = (jax.nn.silu(a) * b).astype(jnp.bfloat16)


def gate_up(x, g, wg, wu, layer):
    n, d = x.shape
    f = wg.shape[2]
    nc = 256
    vm = pl.BlockSpec(memory_space=pltpu.VMEM)
    wspec = pl.BlockSpec((None, d, nc), lambda i: (layer, 0, i))
    return pl.pallas_call(
        gate_kernel, grid=(f // nc,), in_specs=[vm, vm, wspec, wspec],
        out_specs=pl.BlockSpec((n, nc), lambda i: (0, i)),
        out_shape=jax.ShapeDtypeStruct((n, f), jnp.bfloat16),
        scratch_shapes=[pltpu.VMEM((n, d), jnp.bfloat16)],
        cost_estimate=pl.CostEstimate(flops=4 * n * d * f, bytes_accessed=4 * d * f, transcendentals=0),
        compiler_params=pltpu.CompilerParams(vmem_limit_bytes=48 * 1024 * 1024),
        name="gate_up",
    )(x, g, wg, wu)


def attn_kernel(nfull, ncond, diag, first, last, ntp, heads, scale, rb, tk, *refs):
    it = iter(refs)
    bias = next(it)
    q_ref = next(it)
    full = [(next(it), next(it)) for _ in range(nfull)]
    own = (next(it), next(it)) if diag else None
    cond = [(next(it), next(it)) for _ in range(ncond)]
    if not first:
        m_in, l_in, o_in = next(it), next(it), next(it)
    out = next(it)
    if not last:
        m_s, l_s, o_s = out, next(it), next(it)
    nq = q_ref.shape[0]
    rows = range(0, nq, rb)

    def logits(t):
        lo, k_ref, _, off, size, _ = t
        s = lax.dot_general(q_ref[lo:lo + rb, :], k_ref[off:off + size, :], (((1,), (1,)), ((), ())),
                            preferred_element_type=jnp.float32)
        return s * (scale * LOG2E)

    def absorb(t, s, st):
        lo, _, v_ref, off, size, mask = t
        if mask == "causal":
            r = lax.broadcasted_iota(jnp.int32, s.shape, 0) + lo
            c = lax.broadcasted_iota(jnp.int32, s.shape, 1) + off
            s = jnp.where(c <= r, s, -jnp.inf)
        elif mask == "bias":
            s = s + bias[:1, off:off + size]
        mx = jnp.max(s, axis=-1, keepdims=True)
        if st is not None:
            mx = jnp.maximum(mx, st[0])
        p = jnp.exp2(s - mx)
        ps = jnp.sum(p, axis=-1, keepdims=True)
        o = jnp.dot(p.astype(jnp.bfloat16), v_ref[off:off + size, :], preferred_element_type=jnp.float32)
        if st is not None:
            al = jnp.exp2(st[0] - mx)
            ps = ps + al * st[1]
            o = o + al * st[2]
        return mx, ps, o

    def one_head(put):
        st = {lo: None for lo in rows}
        if not first:
            st = {lo: (m_in[lo:lo + rb, :1], l_in[lo:lo + rb, :1], o_in[lo:lo + rb, :]) for lo in rows}
        tiles = [(lo, k, v, off, tk, None) for k, v in full for off in range(0, k.shape[0], tk) for lo in rows]
        if diag:
            tiles += [(lo, own[0], own[1], 0, lo + rb, "causal") for lo in rows]
        tiles += [(lo, k, v, 0, k.shape[0], "bias") for k, v in cond for lo in rows]
        s_next = logits(tiles[0])
        for i, t in enumerate(tiles):
            s = s_next
            if i + 1 < len(tiles):
                s_next = logits(tiles[i + 1])
            st[t[0]] = absorb(t, s, st[t[0]])
        for lo in rows:
            m, l, o = st[lo]
            if last:
                put(lo, (o / l).astype(jnp.bfloat16))
            else:
                m_s[lo:lo + rb, :] = jnp.broadcast_to(m, (rb, 128))
                l_s[lo:lo + rb, :] = jnp.broadcast_to(l, (rb, 128))
                o_s[lo:lo + rb, :] = o

    if ntp == 1:
        def put(lo, v):
            out[lo:lo + rb, :] = v

        one_head(put)
        return

    buf, send_r, send_l, recv_r, recv_l = [next(it) for _ in range(5)]
    z = lax.axis_index("tp")
    step = pl.program_id(0)
    end = ntp - 1
    dh = q_ref.shape[1]

    @pl.when(step == 0)
    def _():
        bar = pltpu.get_barrier_semaphore()

        @pl.when(z > 0)
        def _():
            pl.semaphore_signal(bar, inc=1, device_id={"tp": z - 1}, device_id_type=MESH)

        @pl.when(z < end)
        def _():
            pl.semaphore_signal(bar, inc=1, device_id={"tp": z + 1}, device_id_type=MESH)

        @pl.when((z > 0) & (z < end))
        def _():
            pl.semaphore_wait(bar, 2)

        @pl.when((z == 0) | (z == end))
        def _():
            pl.semaphore_wait(bar, 1)

    def rightwards(src, h):
        return pltpu.make_async_remote_copy(
            src_ref=buf.at[src, h], dst_ref=buf.at[src, h], send_sem=send_r.at[src, h], recv_sem=recv_r.at[src, h],
            device_id={"tp": z + 1}, device_id_type=MESH)

    def leftwards(src, h):
        return pltpu.make_async_remote_copy(
            src_ref=buf.at[src, h], dst_ref=buf.at[src, h], send_sem=send_l.at[src, h], recv_sem=recv_l.at[src, h],
            device_id={"tp": z - 1}, device_id_type=MESH)

    def emit(src, h):
        col = pl.multiple_of((h * ntp + src) * dh, dh)
        out[:, pl.ds(col, dh)] = buf[src, h]

    @pl.when(step < heads)
    def _():
        def put(lo, v):
            buf[z, step, lo:lo + rb, :] = v

        one_head(put)

        @pl.when(z < end)
        def _():
            rightwards(z, step).start()

        @pl.when(z > 0)
        def _():
            leftwards(z, step).start()

        emit(z, step)

    for k in range(1, ntp):
        c = step - k
        live = (c >= 0) & (c < heads)

        @pl.when(live & (z - k >= 0))
        def _():
            rightwards(z - k, c).wait_recv()

            @pl.when(z < end)
            def _():
                rightwards(z - k, c).start()

            emit(z - k, c)

        @pl.when(live & (z + k <= end))
        def _():
            leftwards(z + k, c).wait_recv()

            @pl.when(z > 0)
            def _():
                leftwards(z + k, c).start()

            emit(z + k, c)

    @pl.when(step == pl.num_programs(0) - 1)
    def _():
        def body(h, _):
            for src in range(ntp):
                @pl.when((z >= src) & (z < end))
                def _():
                    rightwards(src, h).wait_send()

                @pl.when((z <= src) & (z > 0))
                def _():
                    leftwards(src, h).wait_send()
            return 0

        lax.fori_loop(0, heads, body, 0)


def attention(bias, q, full, diag, cond, state, last, g, ntp=1, cid=None):
    n, hd = q.shape
    dh = 128
    heads = hd // dh
    first = state is None
    steps = heads if ntp == 1 else heads + ntp - 1
    at = lambda h: jnp.minimum(h, heads - 1)
    args = [bias, q]
    specs = [pl.BlockSpec(memory_space=pltpu.VMEM), pl.BlockSpec((n, dh), lambda h: (0, at(h)))]
    kvspec = lambda t: pl.BlockSpec((t, dh), lambda h: (0, at(h) // g))
    keys = 0
    for k, v in full + ([diag] if diag is not None else []) + cond:
        args += [k, v]
        specs += [kvspec(k.shape[0])] * 2
        keys += k.shape[0]
    hspec = pl.BlockSpec((n, dh), lambda h: (0, at(h)))
    f32 = jax.ShapeDtypeStruct((n, hd), jnp.float32)
    if not first:
        args += list(state)
        specs += [hspec] * 3
    scratch = []
    if ntp > 1:
        out_shape = jax.ShapeDtypeStruct((n, hd * ntp), jnp.bfloat16)
        out_specs = pl.BlockSpec(memory_space=pltpu.VMEM)
        scratch = [pltpu.VMEM((ntp, heads, n, dh), jnp.bfloat16)] + [pltpu.SemaphoreType.DMA((ntp, heads))] * 4
    elif last:
        out_shape, out_specs = jax.ShapeDtypeStruct((n, hd), jnp.bfloat16), hspec
    else:
        out_shape, out_specs = (f32,) * 3, (hspec,) * 3
    kern = functools.partial(attn_kernel, len(full), len(cond), diag is not None, first, last, ntp, heads,
                             dh ** -0.5, 128, 2048)
    extra = dict(collective_id=cid, has_side_effects=True) if ntp > 1 else {}
    return pl.pallas_call(
        kern, grid=(steps,), in_specs=specs, out_specs=out_specs, out_shape=out_shape, scratch_shapes=scratch,
        cost_estimate=pl.CostEstimate(flops=8 * n * hd * keys, bytes_accessed=4 * keys * 256, transcendentals=0),
        compiler_params=pltpu.CompilerParams(vmem_limit_bytes=60 * 1024 * 1024, **extra),
        name="attn_last" if last else "attn_first",
    )(*args)


def proj_kernel(a_ref, w_ref, x_ref, out_ref):
    y = jnp.dot(a_ref[...], w_ref[...], preferred_element_type=jnp.float32)
    out_ref[...] = x_ref[...] + y.astype(jnp.bfloat16)


def proj(a, w, x):
    n, k = a.shape
    d = w.shape[1]
    nc = 256
    col = pl.BlockSpec((n, nc), lambda i: (0, i))
    return pl.pallas_call(
        proj_kernel, grid=(d // nc,),
        in_specs=[pl.BlockSpec(memory_space=pltpu.VMEM), pl.BlockSpec((k, nc), lambda i: (0, i)), col],
        out_specs=col, out_shape=jax.ShapeDtypeStruct((n, d), jnp.bfloat16),
        cost_estimate=pl.CostEstimate(flops=2 * n * k * d, bytes_accessed=2 * k * d, transcendentals=0),
        compiler_params=pltpu.CompilerParams(vmem_limit_bytes=48 * 1024 * 1024),
        name="proj",
    )(a, w, x)


def sum_kernel(ntp, nb, rsplit, skew, a_ref, w_ref, x_ref, out_ref, p_ref, ra, rb_, ga, gb, send_sem, recv_sem):
    z = lax.axis_index("tp")
    s = pl.program_id(0)
    nc = w_ref.shape[1]
    half = a_ref.shape[0] // 2
    rows = half // rsplit
    nchunk = nb * rsplit
    last = ntp - 1

    @pl.when(s == 0)
    def _():
        bar = pltpu.get_barrier_semaphore()

        @pl.when(z > 0)
        def _():
            pl.semaphore_signal(bar, inc=1, device_id={"tp": z - 1}, device_id_type=MESH)

        @pl.when(z < last)
        def _():
            pl.semaphore_signal(bar, inc=1, device_id={"tp": z + 1}, device_id_type=MESH)

        @pl.when((z > 0) & (z < last))
        def _():
            pl.semaphore_wait(bar, 2)

        @pl.when((z == 0) | (z == last))
        def _():
            pl.semaphore_wait(bar, 1)

    @pl.when((s < nchunk) & (s % rsplit == 0))
    def _():
        p = jnp.dot(a_ref[...], w_ref[...], preferred_element_type=jnp.float32)
        for h in range(2):
            for r in range(rsplit):
                lo = h * half + r * rows
                p_ref[h, s + r] = p[lo:lo + rows, :]

    def copy(kind, src, dst, c, to):
        return pltpu.make_async_remote_copy(
            src_ref=src.at[c], dst_ref=dst.at[c], send_sem=send_sem.at[kind, c], recv_sem=recv_sem.at[kind, c],
            device_id={"tp": to}, device_id_type=MESH)

    def side(h, red, gat):
        d = (last - z) if h == 0 else z
        to_end = (z - 1) if h == 0 else (z + 1)
        from_end = (z + 1) if h == 0 else (z - 1)

        def store(c, v):
            col = pl.multiple_of((c // rsplit) * nc, nc)
            row = pl.multiple_of(h * half + (c % rsplit) * rows, rows)
            out_ref[pl.ds(row, rows), pl.ds(col, nc)] = v

        c = s - skew * d

        @pl.when((c >= 0) & (c < nchunk))
        def _():
            @pl.when(d == 0)
            def _():
                copy(h, p_ref.at[h], red, c, to_end).start()

            @pl.when((d > 0) & (d < last))
            def _():
                copy(h, red, red, c, to_end).wait_recv()
                red[c] = red[c] + p_ref[h, c]
                copy(h, red, red, c, to_end).start()

            @pl.when(d == last)
            def _():
                copy(h, red, red, c, from_end).wait_recv()
                col = pl.multiple_of((c // rsplit) * nc, nc)
                row = pl.multiple_of(h * half + (c % rsplit) * rows, rows)
                y = (red[c] + p_ref[h, c]).astype(jnp.bfloat16)
                xn = x_ref[pl.ds(row, rows), pl.ds(col, nc)] + y
                gat[c] = xn
                copy(2 + h, gat, gat, c, from_end).start()
                store(c, xn)

        e = s - skew * (2 * last - d)

        @pl.when((e >= 0) & (e < nchunk) & (d < last))
        def _():
            copy(2 + h, gat, gat, e, from_end).wait_recv()

            @pl.when(d > 0)
            def _():
                copy(2 + h, gat, gat, e, from_end).start()

            store(e, gat[e])

    side(0, ra, ga)
    side(1, rb_, gb)

    @pl.when(s == pl.num_programs(0) - 1)
    def _():
        def body(c, _):
            for h, (red, gat) in enumerate(((ra, ga), (rb_, gb))):
                d = (last - z) if h == 0 else z
                to_end = (z - 1) if h == 0 else (z + 1)
                from_end = (z + 1) if h == 0 else (z - 1)

                @pl.when(d < last)
                def _():
                    copy(h, red, red, c, to_end).wait_send()

                @pl.when(d > 0)
                def _():
                    copy(2 + h, gat, gat, c, from_end).wait_send()
            return 0

        lax.fori_loop(0, nchunk, body, 0)


def matmul_sum(a, w, layer, x, ntp, cid):
    n, k = a.shape
    d = w.shape[2]
    nc, rsplit, skew = 256, 2, 2
    nb = d // nc
    nchunk = nb * rsplit
    rows = n // 2 // rsplit
    steps = nchunk + 2 * (ntp - 1) * skew
    kern = functools.partial(sum_kernel, ntp, nb, rsplit, skew)
    vm = pl.BlockSpec(memory_space=pltpu.VMEM)
    f32, bf = jnp.float32, jnp.bfloat16
    return pl.pallas_call(
        kern, grid=(steps,),
        in_specs=[vm, pl.BlockSpec((None, k, nc), lambda s: (layer, 0, jnp.minimum(s // rsplit, nb - 1))), vm],
        out_specs=vm,
        out_shape=jax.ShapeDtypeStruct((n, d), bf),
        scratch_shapes=[
            pltpu.VMEM((2, nchunk, rows, nc), f32),
            pltpu.VMEM((nchunk, rows, nc), f32),
            pltpu.VMEM((nchunk, rows, nc), f32),
            pltpu.VMEM((nchunk, rows, nc), bf),
            pltpu.VMEM((nchunk, rows, nc), bf),
            pltpu.SemaphoreType.DMA((4, nchunk)),
            pltpu.SemaphoreType.DMA((4, nchunk)),
        ],
        cost_estimate=pl.CostEstimate(flops=100_000_000_000, bytes_accessed=2 * k * d, transcendentals=0),
        compiler_params=pltpu.CompilerParams(
            collective_id=cid, has_side_effects=True, vmem_limit_bytes=62 * 1024 * 1024),
        name="matmul_sum",
    )(a, w, x)


def solution(mesh):
    sp = mesh.shape['sp']
    tp = mesh.shape['tp']
    row = ('dp', 'sp')
    kv_spec = P(None, row, 'tp', None)
    col = P(None, None, 'tp')
    rowsplit = P(None, 'tp', None)

    def xchg(t, bit):
        return lax.ppermute(t, 'sp', [(i, i ^ bit) for i in range(sp)])

    def body(x, pos, k_hist, v_hist, wq, wk, wv, wo, wg, wu, wd, g1, g2):
        n, d = x.shape
        layers, t, kvl, dh = k_hist.shape
        hql = wq.shape[-1] // dh
        g = hql // kvl
        idx = lax.axis_index('sp')
        src = jnp.arange(3 * n, dtype=jnp.int32)[None, :] // n + 1
        bias = jnp.where((idx ^ src) < idx, 0.0, -jnp.inf).astype(jnp.float32)
        bias = jnp.broadcast_to(bias, (8, 3 * n))
        tabs = rope_tables(pos, dh)
        plane = lax.axis_index('dp') * sp + idx
        nplane = mesh.shape['dp'] * sp
        plane = lax.axis_index('dp') * sp + idx
        nplane = mesh.shape['dp'] * sp
        raw = [(k_hist[l].reshape(t, kvl * dh), v_hist[l].reshape(t, kvl * dh)) for l in range(layers)]

        def fetch(k0, v0):
            k1, v1 = xchg(k0, 1), xchg(v0, 1)
            k2, v2 = xchg(k0, 2), xchg(v0, 2)
            return k1, v1, k2, v2

        def whole_wo(l):
            part = lax.dynamic_slice(wo, (l, plane * dh, 0), (1, dh, d))[0]
            w = lax.all_gather(part, 'tp', axis=0)
            return lax.all_gather(w, ('dp', 'sp'), axis=0).reshape(tp * hql * dh, d)

        near = fetch(*raw[0])
        full_wo = {l: whole_wo(l) for l in range(1, layers)} if nplane == hql else {}
        far = None
        ks, vs = [], []
        for l in range(layers):
            k0, v0 = raw[l]
            k1, v1, k2, v2 = near
            q, k, v = qkv(x, g1[l:l + 1], *tabs, wq, wk, wv, l, dh)
            ks.append(k.reshape(n, kvl, dh))
            vs.append(v.reshape(n, kvl, dh))
            n1, w1 = xchg(k, 1), xchg(v, 1)
            n2, w2 = xchg(k, 2), xchg(v, 2)
            st = attention(bias, q, [(k0, v0), (k1, v1)], (k, v), [], None, False, g)
            k2, v2, n2, w2, st = lax.optimization_barrier((k2, v2, n2, w2, st))
            k3, v3 = far if far is not None else (xchg(k2, 1), xchg(v2, 1))
            n3, w3 = xchg(n2, 1), xchg(w2, 1)
            late = [(jnp.concatenate([n1, n2, n3]), jnp.concatenate([w1, w2, w3]))]
            last = [(k2, v2), (k3, v3)]
            more = l + 1 < layers
            net = (tp, 2 * l) if l in full_wo else ()
            attn = attention(bias, q, last, None, late, st, True, g, *net)
            if more:
                *raw[l + 1], attn = lax.optimization_barrier((*raw[l + 1], attn))
                near = fetch(*raw[l + 1])
            x = proj(attn, full_wo[l], x) if l in full_wo else matmul_sum(attn, wo, l, x, tp, 2 * l)
            if more:
                *near, x = lax.optimization_barrier((*near, x))
                far = xchg(near[2], 1), xchg(near[3], 1)
            u = gate_up(x, g2[l:l + 1], wg, wu, l)
            if more:
                *far, u = lax.optimization_barrier((*far, u))
            x = matmul_sum(u, wd, l, x, tp, 2 * l + 1)
        return x, jnp.stack(ks), jnp.stack(vs)

    in_specs = (P(row, None), P(row), kv_spec, kv_spec, col, col, col, rowsplit, col, col, rowsplit, P(), P())
    out_specs = (P(row, None), kv_spec, kv_spec)
    return jax.shard_map(body, mesh=mesh, in_specs=in_specs, out_specs=out_specs, check_vma=False)
```

time: 2180 us -> 1010 us (0.46)
  blocking collectives: 1130 us -> 0 us
  Pallas kernels: 0 us -> 806 us
  matrix products: 463 us -> 0 us
  other arithmetic: 168 us -> 8.11 us
  local copies, waits for them, and re-layouts: 159 us -> 28.3 us
  waiting for transfers between devices: 225 us -> 132 us
    psum x4 -> x0, blocking collectives: 1130 us -> none  [the longest x2 575 us: body(): x = x + lax.psum(mm(attn, wo[l]), 'tp').astype(jnp.bfloat16)]
    pallas_call x0 -> x12, Pallas kernels: none -> 806 us  [the longest x3 482 us: matmul_sum(): pl.pallas_call(kern, grid=(steps,), in_specs=[vm, pl.BlockSpec((None, k,...]
    dot_general x174 -> x0, matrix products: 463 us -> none  [the longest x14 196 us: mm(): return jnp.dot(a, b, preferred_element_type=jnp.float32)]
    reduce_scatter x2 -> x0, waiting for transfers between devices: 107 us -> none  [body(): lax.psum_scatter(o_h.reshape(s_tot, kvl, g, dh) * sc[..., None], 'sp', sc...]
    reduce_sum x84 -> x0, other arithmetic: 94.5 us -> none  [the longest x80 71.1 us: partial_attn(): return (m, jnp.sum(p, axis=-1), o)]
    dynamic_update_slice x160 -> x0, local copies, waits for them, and re-layouts: 92.3 us -> none  [the longest x128 91.2 us: body(): m_h, l_h, o_h = lax.map(lambda qq: partial_attn(qq, kh, vh), q_all)]
    ppermute x0 -> x24, waiting for transfers between devices: none -> 48.3 us  [xchg(): return lax.ppermute(t, 'sp', [(i, i ^ bit) for i in range(sp)])]
    pmax x2 -> x0, waiting for transfers between devices: 47.2 us -> none  [body(): m_g = lax.pmax(m_h, 'sp')]
  transfers between devices with their start and end apart: 12 -> 26, of which waited for: 8 -> 4; matrix products, arithmetic and copies ran while one was open for 8% -> 2% of each run, Pallas kernels for 0% -> 58%
where the time goes in v1:
time: 1010 us; the launch traced here: 1000 us
  Pallas kernels  806 us (80%)
  waiting for transfers between devices  132 us (13%)
  local copies, waits for them, and re-layouts  28.3 us (3%)
  between operations  14.6 us (1%)
  starting transfers between devices  11.4 us (1%)
    pallas_call x3, Pallas kernels, matmul_sum(): pl.pallas_call(kern, grid=(steps,), in_specs=[vm, pl.BlockSpec((None, k,...  482 us
    pallas_call x4, Pallas kernels, attention(): pl.pallas_call(kern, grid=(steps,), in_specs=specs, out_specs=out_specs,...  188 us
    all_gather x1, waiting for transfers between devices, whole_wo(): w = lax.all_gather(part, 'tp', axis=0)  84 us
    pallas_call x2, Pallas kernels, gate_up(): pl.pallas_call(gate_kernel, grid=(f // nc,), in_specs=[vm, vm, wspec, wsp...  78.3 us
    ppermute x24, waiting for transfers between devices, xchg(): return lax.ppermute(t, 'sp', [(i, i ^ bit) for i in range(sp)])  48.3 us
    pallas_call x2, Pallas kernels, qkv(): pl.pallas_call(functools.partial(qkv_kernel, nq, dh), grid=(nq + 2,), in_...  31.8 us
    pallas_call x1, Pallas kernels, proj(): pl.pallas_call(proj_kernel, grid=(d // nc,), in_specs=[pl.BlockSpec(memor...  26.3 us
  transfers between devices with their start and end apart: 26, of which 4 were waited for; matrix products, arithmetic and copies ran while one was open for 2% of the time, Pallas kernels for 58%

profile of v1, /device:TPU:0, one launch (start us, length us, event | category | flops | bytes accessed | tf_op | source)
XLA Modules:
  0.0 1001.1 jit_solution(1370866842519225188)
XLA Ops:
  7.2 2.3 constant_dynamic-slice_fusion
  9.6 84.0 %all-gather.4.cloned.1.call-done = bf16[4,128,4096]{2,1,0:T(8,128)(2,1)} async-done(((bf16[1,128,4096]{2,1,0:T(8,128)(2,1)}), bf16[4,128,4096]{2,1,0:T(8,128)(2,1)}) %all-gather.4.cloned.1.call-update) | async-done | bytes 4194320 | tf_op jit(solution)/shard_map/all_gather | solution.py:519
  93.6 1.6 copy-done.16
  95.2 1.5 fusion.9
  96.7 1.1 copy.25
  97.8 1.5 collective-permute-start
  99.3 2.2 fusion.8
  101.6 1.1 copy.24
  102.7 0.2 collective-permute-start.5
  102.9 0.6 collective-permute-start.1
  103.5 1.0 fusion
  104.5 0.2 pad_maximum_fusion.6
  104.8 16.9 %qkv.2 = (bf16[512,1024]{1,0:T(8,128)(2,1)S(1)}, bf16[512,256]{1,0:T(8,128)(2,1)S(1)}, bf16[512,256]{1,0:T(8,128)(2,1)S(1)}) custom-call(bf16[512,4096]{1,0:T(8,128)(2,1)} %x_ref.3, bf16[1,4096]{1,0:T(2,128)(2,1)S(1)} %get-tuple-element.84.g_ref, f32[512,128]{1,0:T(8,128)S(1)} %get-tuple-element.88.c_ref, f32[512,128]{1,0:T(8,128)S(1)} %get-tuple-element.89.s_ref, ...), custom_call_target="tpu_custom_call" | custom-call | flops 6442450944 | bytes 8388608 | tf_op jit(solution)/shard_map/qkv/pallas_call | solution.py:68
  121.7 0.9 copy-done.13
  122.7 1.4 collective-permute-start.3
  124.2 0.1 collective-permute-start.10
  124.2 0.7 collective-permute-start.2
  125.0 0.2 copy-done.23
  125.1 0.3 copy-done.24
  125.5 0.6 broadcast_in_dim.18.refs_0_
  126.1 32.2 %attn_first.2 = (f32[512,1024]{1,0:T(8,128)}, f32[512,1024]{1,0:T(8,128)}, f32[512,1024]{1,0:T(8,128)}) custom-call(f32[8,1536]{1,0:T(8,128)} %broadcast_in_dim.18.refs_0_, bf16[512,1024]{1,0:T(8,128)(2,1)} %copy-done.13, bf16[2048,256]{1,0:T(8,128)(2,1)} %bitcast.18.refs_2_, bf16[2048,256]{1,0:T(8,128)(2,1)} %bitcast.17.refs_3_, ...), custom_call_target="tpu_custom_call" | custom-call | flops 19327352832 | bytes 4718592 | tf_op jit(solution)/shard_map/attn_first/pallas_call | solution.py:313
  158.3 44.0 %collective-permute-done.2 = bf16[512,256]{1,0:T(8,128)(2,1)S(1)} collective-permute-done((bf16[512,256]{1,0:T(8,128)(2,1)S(1)}, bf16[512,256]{1,0:T(8,128)(2,1)S(1)}, u32[]{:S(2)}, u32[]{:S(2)}) %collective-permute-start.2) | collective-permute-done | bytes 262176 | tf_op jit(solution)/shard_map/ppermute | solution.py:494
  202.3 0.6 collective-permute-start.11
  202.9 0.1 collective-permute-start.9
  202.9 0.4 collective-permute-start.6
  203.4 0.1 collective-permute-start.7
  203.5 1.7 copy_bitcast_fusion.2
  205.2 0.9 pad_maximum_fusion.1.refs_7_
  206.1 0.9 pad_maximum_fusion.refs_6_
  207.1 1.3 collective-permute-done.6.refs_4_
  208.4 3.0 collective-permute-done.7.refs_5_
  211.4 41.1 %attn_last.2.a_ref = bf16[512,1024]{1,0:T(8,128)(2,1)} custom-call(f32[8,1536]{1,0:T(8,128)} %broadcast_in_dim.18.refs_0_, bf16[512,1024]{1,0:T(8,128)(2,1)} %copy-done.13, bf16[2048,256]{1,0:T(8,128)(2,1)} %collective-permute-done.refs_2_, bf16[2048,256]{1,0:T(8,128)(2,1)} %collective-permute-done.1.refs_3_, ...), custom_call_target="tpu_custom_call" | custom-call | flops 23622320128 | bytes 5767168 | tf_op jit(solution)/shard_map/attn_last/pallas_call | solution.py:313
  252.5 0.1 collective-permute-start.12
  252.6 1.3 collective-permute-start.14
  253.8 0.1 collective-permute-start.13
  254.0 0.8 collective-permute-start.15
  254.7 160.3 %matmul_sum.3.x_ref = bf16[512,4096]{1,0:T(8,128)(2,1)} custom-call(bf16[512,1024]{1,0:T(8,128)(2,1)} %attn_last.2.a_ref, bf16[2,1024,4096]{2,1,0:T(8,128)(2,1)} %w_ref.3, bf16[512,4096]{1,0:T(8,128)(2,1)} %x_ref.3), custom_call_target="tpu_custom_call" | custom-call | flops 99999997952 | bytes 8388608 | tf_op jit(solution)/shard_map/matmul_sum/pallas_call | solution.py:464
  415.0 0.1 collective-permute-start.16
  415.1 0.5 collective-permute-start.17
  415.6 39.2 %gate_up.2.a_ref = bf16[512,3584]{1,0:T(8,128)(2,1)S(1)} custom-call(bf16[512,4096]{1,0:T(8,128)(2,1)} %matmul_sum.3.x_ref, bf16[1,4096]{1,0:T(2,128)(2,1)S(1)} %get-tuple-element.82.g_ref, bf16[2,4096,3584]{2,1,0:T(8,128)(2,1)} %wg_ref.3, bf16[2,4096,3584]{2,1,0:T(8,128)(2,1)} %wu_ref.3), custom_call_target="tpu_custom_call" | custom-call | flops 30064771072 | bytes 58720256 | tf_op jit(solution)/shard_map/gate_up/pallas_call | solution.py:102
  454.8 1.8 copy-done.1
  456.7 1.0 copy-done.22
  457.6 159.6 %matmul_sum.4.x_ref = bf16[512,4096]{1,0:T(8,128)(2,1)} custom-call(bf16[512,3584]{1,0:T(8,128)(2,1)} %copy-done.1, bf16[2,3584,4096]{2,1,0:T(8,128)(2,1)} %w_ref.5, bf16[512,4096]{1,0:T(8,128)(2,1)} %matmul_sum.3.x_ref), custom_call_target="tpu_custom_call" | custom-call | flops 99999997952 | bytes 29360128 | tf_op jit(solution)/shard_map/matmul_sum/pallas_call | solution.py:464
  617.2 14.9 %qkv.3 = (bf16[512,1024]{1,0:T(8,128)(2,1)S(1)}, bf16[512,256]{1,0:T(8,128)(2,1)S(1)}, bf16[512,256]{1,0:T(8,128)(2,1)S(1)}) custom-call(bf16[512,4096]{1,0:T(8,128)(2,1)} %matmul_sum.4.x_ref, bf16[1,4096]{1,0:T(2,128)(2,1)S(1)} %get-tuple-element.83.g_ref, f32[512,128]{1,0:T(8,128)S(1)} %copy-done.4, f32[512,128]{1,0:T(8,128)S(1)} %copy-done.6, ...), custom_call_target="tpu_custom_call" | custom-call | flops 6442450944 | bytes 8388608 | tf_op jit(solution)/shard_map/qkv/pallas_call | solution.py:68
  632.1 1.0 copy-done.14
  633.1 1.5 collective-permute-start.19
  634.6 0.5 collective-permute-start.18
  635.1 32.4 %attn_first.3 = (f32[512,1024]{1,0:T(8,128)}, f32[512,1024]{1,0:T(8,128)}, f32[512,1024]{1,0:T(8,128)}) custom-call(f32[8,1536]{1,0:T(8,128)} %broadcast_in_dim.18.refs_0_, bf16[512,1024]{1,0:T(8,128)(2,1)} %copy-done.14, bf16[2048,256]{1,0:T(8,128)(2,1)} %get-tuple-element.53.refs_2_, bf16[2048,256]{1,0:T(8,128)(2,1)} %get-tuple-element.54.refs_3_, ...), custom_call_target="tpu_custom_call" | custom-call | flops 19327352832 | bytes 4718592 | tf_op jit(solution)/shard_map/attn_first/pallas_call | solution.py:313
  667.5 0.3 collective-permute-start.23
  668.0 0.3 collective-permute-start.20
  668.3 1.0 stack_reshape.13
  669.3 1.0 stack_reshape.15
  670.4 1.6 pad_maximum_fusion.4
  671.9 0.2 collective-permute-start.21
  672.1 1.6 pad_maximum_fusion.5
  673.7 0.9 pad_maximum_fusion.3.refs_7_
  674.7 1.0 pad_maximum_fusion.2.refs_6_
  675.6 82.5 %attn_last.3.a_ref = bf16[512,4096]{1,0:T(8,128)(2,1)} custom-call(f32[8,1536]{1,0:T(8,128)} %broadcast_in_dim.18.refs_0_, bf16[512,1024]{1,0:T(8,128)(2,1)} %copy-done.14, bf16[2048,256]{1,0:T(8,128)(2,1)} %copy-done.21, bf16[2048,256]{1,0:T(8,128)(2,1)} %collective-permute-done.15.refs_3_, bf16[2048,256]{1,0:T(8,128)(2,1)} %copy-done.22, ...), custom_call_target="tpu_custom_call" | custom-call | flops 23622320128 | bytes 5767168 | tf_op jit(solution)/shard_map/attn_last/pallas_call | solution.py:313
  758.2 26.3 %proj.1.x_ref = bf16[512,4096]{1,0:T(8,128)(2,1)S(1)} custom-call(bf16[512,4096]{1,0:T(8,128)(2,1)} %attn_last.3.a_ref, bf16[4096,4096]{1,0:T(8,128)(2,1)} %bitcast.23, bf16[512,4096]{1,0:T(8,128)(2,1)} %matmul_sum.4.x_ref), custom_call_target="tpu_custom_call" | custom-call | flops 17179869184 | bytes 33554432 | tf_op jit(solution)/shard_map/proj/pallas_call | solution.py:331
  784.5 2.0 copy-done
  786.5 39.1 %gate_up.3.a_ref = bf16[512,3584]{1,0:T(8,128)(2,1)S(1)} custom-call(bf16[512,4096]{1,0:T(8,128)(2,1)} %copy-done, bf16[1,4096]{1,0:T(2,128)(2,1)S(1)} %get-tuple-element.81.g_ref, bf16[2,4096,3584]{2,1,0:T(8,128)(2,1)} %wg_ref.3, bf16[2,4096,3584]{2,1,0:T(8,128)(2,1)} %wu_ref.3), custom_call_target="tpu_custom_call" | custom-call | flops 30064771072 | bytes 58720256 | tf_op jit(solution)/shard_map/gate_up/pallas_call | solution.py:102
  825.6 1.9 copy-done.2
  827.5 161.9 %matmul_sum.5 = bf16[512,4096]{1,0:T(8,128)(2,1)} custom-call(bf16[512,3584]{1,0:T(8,128)(2,1)} %copy-done.2, bf16[2,3584,4096]{2,1,0:T(8,128)(2,1)} %w_ref.5, bf16[512,4096]{1,0:T(8,128)(2,1)} %copy-done), custom_call_target="tpu_custom_call" | custom-call | flops 99999997952 | bytes 29360128 | tf_op jit(solution)/shard_map/matmul_sum/pallas_call | solution.py:464
  989.4 4.7 copy.27
  (77 shorter events, 0.5 us)
Async XLA Ops:
  7.2 86.4 %all-gather.4.cloned.1.call-start = ((), (), s32[]{:S(2)}) async-start(), calls=%async_computation | async-start | bytes 5242880 | tf_op jit(solution)/shard_map/all_gather | solution.py:519
  9.5 748.6 %all-gather.6.cloned.1.call-start = ((), (), s32[]{:S(2)}) async-start(), calls=%async_computation.1 | async-start | bytes 37748736 | tf_op jit(solution)/shard_map/all_gather | solution.py:520
  93.6 1.6 copy-start.16
  96.7 2.6 copy-start.17
  97.8 26.3 %collective-permute-start.4 = (bf16[2048,256]{1,0:T(8,128)(2,1)}, bf16[2048,256]{1,0:T(8,128)(2,1)S(1)}, u32[]{:S(2)}, u32[]{:S(2)}) collective-permute-start(bf16[2048,256]{1,0:T(8,128)(2,1)} %bitcast.18.refs_2_), channel_id=1, source_target_pairs={{0,1},{1,0},{2,3},{3,2},{4,5},{5,4},{6,7},{7,6},{8,9},{9,8},{10,11... | collective-permute-start | bytes 3145736 | tf_op jit(solution)/shard_map/ppermute | solution.py:494
  97.8 104.4 %collective-permute-start = (bf16[2048,256]{1,0:T(8,128)(2,1)}, bf16[2048,256]{1,0:T(8,128)(2,1)}, u32[]{:S(2)}, u32[]{:S(2)}) collective-permute-start(bf16[2048,256]{1,0:T(8,128)(2,1)} %bitcast.18.refs_2_), channel_id=1, source_target_pairs={{0,2},{1,3},{2,0},{3,1},{4,6},{5,7},{6,4},{7,5},{8,10},{9,11},{10,... | collective-permute-start | bytes 3145736 | tf_op jit(solution)/shard_map/ppermute | solution.py:494
  101.6 2.0 copy-start.20
  101.6 3.2 copy-start.18
  102.7 21.5 %collective-permute-start.5 = (bf16[2048,256]{1,0:T(8,128)(2,1)}, bf16[2048,256]{1,0:T(8,128)(2,1)S(1)}, u32[]{:S(2)}, u32[]{:S(2)}) collective-permute-start(bf16[2048,256]{1,0:T(8,128)(2,1)} %bitcast.17.refs_3_), channel_id=1, source_target_pairs={{0,1},{1,0},{2,3},{3,2},{4,5},{5,4},{6,7},{7,6},{8,9},{9,8},{10,11... | collective-permute-start | bytes 3145736 | tf_op jit(solution)/shard_map/ppermute | solution.py:494
  102.9 99.3 %collective-permute-start.1 = (bf16[2048,256]{1,0:T(8,128)(2,1)}, bf16[2048,256]{1,0:T(8,128)(2,1)}, u32[]{:S(2)}, u32[]{:S(2)}) collective-permute-start(bf16[2048,256]{1,0:T(8,128)(2,1)} %bitcast.17.refs_3_), channel_id=1, source_target_pairs={{0,2},{1,3},{2,0},{3,1},{4,6},{5,7},{6,4},{7,5},{8,10},{9,11},{10,... | collective-permute-start | bytes 3145736 | tf_op jit(solution)/shard_map/ppermute | solution.py:494
  104.8 17.0 %copy-start.3 = (f32[512,128]{1,0:T(8,128)}, f32[512,128]{1,0:T(8,128)S(1)}, u32[]{:S(2)}) copy-start(f32[512,128]{1,0:T(8,128)S(1)} %get-tuple-element.88.c_ref) | copy-start | bytes 786436
  104.8 17.0 %copy-start.5 = (f32[512,128]{1,0:T(8,128)}, f32[512,128]{1,0:T(8,128)S(1)}, u32[]{:S(2)}) copy-start(f32[512,128]{1,0:T(8,128)S(1)} %get-tuple-element.89.s_ref) | copy-start | bytes 786436
  104.8 19.3 %copy-start.19 = (bf16[2,4096]{1,0:T(2,128)(2,1)S(1)}, bf16[2,4096]{1,0:T(2,128)(2,1)}, u32[]{:S(2)}) copy-start(bf16[2,4096]{1,0:T(2,128)(2,1)} %param.25) | copy-start | bytes 49156
  121.7 1.0 copy-start.13
  122.7 3.4 copy-start.7
  122.7 3.4 copy-start.9
  122.7 79.6 %collective-permute-start.3 = (bf16[512,256]{1,0:T(8,128)(2,1)S(1)}, bf16[512,256]{1,0:T(8,128)(2,1)S(1)}, u32[]{:S(2)}, u32[]{:S(2)}) collective-permute-start(bf16[512,256]{1,0:T(8,128)(2,1)S(1)} %get-tuple-element.42.refs_7_), channel_id=1, source_target_pairs={{0,2},{1,3},{2,0},{3,1},{4,6},{5,7},{6,4},{7,5},{8,10},{9,11},{10,... | collective-permute-start | bytes 786440 | tf_op jit(solution)/shard_map/ppermute | solution.py:494
  124.1 1.0 copy-start.23
  124.2 79.2 %collective-permute-start.10 = (bf16[512,256]{1,0:T(8,128)(2,1)S(1)}, bf16[512,256]{1,0:T(8,128)(2,1)S(1)}, u32[]{:S(2)}, u32[]{:S(2)}) collective-permute-start(bf16[512,256]{1,0:T(8,128)(2,1)S(1)} %get-tuple-element.42.refs_7_), channel_id=1, source_target_pairs={{0,1},{1,0},{2,3},{3,2},{4,5},{5,4},{6,7},{7,6},{8,9},{9,8},{10,11... | collective-permute-start | bytes 786440 | tf_op jit(solution)/shard_map/ppermute | solution.py:494
  124.2 1.2 copy-start.24
  124.2 78.0 %collective-permute-start.2 = (bf16[512,256]{1,0:T(8,128)(2,1)S(1)}, bf16[512,256]{1,0:T(8,128)(2,1)S(1)}, u32[]{:S(2)}, u32[]{:S(2)}) collective-permute-start(bf16[512,256]{1,0:T(8,128)(2,1)S(1)} %get-tuple-element.41.refs_6_), channel_id=1, source_target_pairs={{0,2},{1,3},{2,0},{3,1},{4,6},{5,7},{6,4},{7,5},{8,10},{9,11},{10,... | collective-permute-start | bytes 786440 | tf_op jit(solution)/shard_map/ppermute | solution.py:494
  126.1 77.4 %copy-start.15 = (bf16[1,2048,2,128]{3,2,1,0:T(2,128)(2,1)S(1)}, bf16[1,2048,2,128]{3,2,1,0:T(2,128)(2,1)}, u32[]{:S(2)}) copy-start(bf16[1,2048,2,128]{3,2,1,0:T(2,128)(2,1)} %get-tuple-element.78) | copy-start | bytes 3145732
  202.3 3.9 collective-permute-start.8
  202.3 2.9 collective-permute-start.11
  202.9 3.3 collective-permute-start.9
  202.9 5.4 collective-permute-start.6
  203.4 8.0 collective-permute-start.7
  252.5 162.5 %collective-permute-start.12 = (bf16[2048,256]{1,0:T(8,128)(2,1)}, bf16[2048,256]{1,0:T(8,128)(2,1)}, u32[]{:S(2)}, u32[]{:S(2)}) collective-permute-start(bf16[2048,256]{1,0:T(8,128)(2,1)} %get-tuple-element.53.refs_2_), channel_id=1, source_target_pairs={{0,1},{1,0},{2,3},{3,2},{4,5},{5,4},{6,7},{7,6},{8,9},{9,8},{10,11... | collective-permute-start | bytes 3145736 | tf_op jit(solution)/shard_map/ppermute | solution.py:494
  252.6 162.4 %collective-permute-start.14 = (bf16[2048,256]{1,0:T(8,128)(2,1)}, bf16[2048,256]{1,0:T(8,128)(2,1)S(1)}, u32[]{:S(2)}, u32[]{:S(2)}) collective-permute-start(bf16[2048,256]{1,0:T(8,128)(2,1)} %get-tuple-element.53.refs_2_), channel_id=1, source_target_pairs={{0,2},{1,3},{2,0},{3,1},{4,6},{5,7},{6,4},{7,5},{8,10},{9,11},{10,... | collective-permute-start | bytes 3145736 | tf_op jit(solution)/shard_map/ppermute | solution.py:494
  253.8 161.1 %collective-permute-start.13 = (bf16[2048,256]{1,0:T(8,128)(2,1)}, bf16[2048,256]{1,0:T(8,128)(2,1)}, u32[]{:S(2)}, u32[]{:S(2)}) collective-permute-start(bf16[2048,256]{1,0:T(8,128)(2,1)} %get-tuple-element.54.refs_3_), channel_id=1, source_target_pairs={{0,1},{1,0},{2,3},{3,2},{4,5},{5,4},{6,7},{7,6},{8,9},{9,8},{10,11... | collective-permute-start | bytes 3145736 | tf_op jit(solution)/shard_map/ppermute | solution.py:494
  254.0 161.1 %collective-permute-start.15 = (bf16[2048,256]{1,0:T(8,128)(2,1)}, bf16[2048,256]{1,0:T(8,128)(2,1)}, u32[]{:S(2)}, u32[]{:S(2)}) collective-permute-start(bf16[2048,256]{1,0:T(8,128)(2,1)} %get-tuple-element.54.refs_3_), channel_id=1, source_target_pairs={{0,2},{1,3},{2,0},{3,1},{4,6},{5,7},{6,4},{7,5},{8,10},{9,11},{10,... | collective-permute-start | bytes 3145736 | tf_op jit(solution)/shard_map/ppermute | solution.py:494
  415.0 39.8 %copy-start.21 = (bf16[2048,256]{1,0:T(8,128)(2,1)}, bf16[2048,256]{1,0:T(8,128)(2,1)S(1)}, u32[]{:S(2)}) copy-start(bf16[2048,256]{1,0:T(8,128)(2,1)S(1)} %collective-permute-done.14.refs_2_) | copy-start | bytes 3145732
  415.0 41.6 %collective-permute-start.16 = (bf16[2048,256]{1,0:T(8,128)(2,1)S(1)}, bf16[2048,256]{1,0:T(8,128)(2,1)S(1)}, u32[]{:S(2)}, u32[]{:S(2)}) collective-permute-start(bf16[2048,256]{1,0:T(8,128)(2,1)S(1)} %collective-permute-done.14.refs_2_), channel_id=1, source_target_pairs={{0,1},{1,0},{2,3},{3,2},{4,5},{5,4},{6,7},{7,6},{8,9},{9,8},{10,11... | collective-permute-start | bytes 3145736 | tf_op jit(solution)/shard_map/ppermute | solution.py:494
  415.1 42.5 %collective-permute-start.17 = (bf16[2048,256]{1,0:T(8,128)(2,1)}, bf16[2048,256]{1,0:T(8,128)(2,1)}, u32[]{:S(2)}, u32[]{:S(2)}) collective-permute-start(bf16[2048,256]{1,0:T(8,128)(2,1)} %collective-permute-done.15.refs_3_), channel_id=1, source_target_pairs={{0,1},{1,0},{2,3},{3,2},{4,5},{5,4},{6,7},{7,6},{8,9},{9,8},{10,11... | collective-permute-start | bytes 3145736 | tf_op jit(solution)/shard_map/ppermute | solution.py:494
  454.8 1.8 copy-start.1
  456.6 160.5 %copy-start.4 = (f32[512,128]{1,0:T(8,128)S(1)}, f32[512,128]{1,0:T(8,128)}, u32[]{:S(2)}) copy-start(f32[512,128]{1,0:T(8,128)} %copy-done.3) | copy-start | bytes 786436
  456.6 160.5 %copy-start.6 = (f32[512,128]{1,0:T(8,128)S(1)}, f32[512,128]{1,0:T(8,128)}, u32[]{:S(2)}) copy-start(f32[512,128]{1,0:T(8,128)} %copy-done.5) | copy-start | bytes 786436
  456.6 1.0 copy-start.22
  632.1 1.0 copy-start.14
  633.1 2.0 copy-start.11
  633.1 2.0 copy-start.12
  633.1 34.4 %collective-permute-start.19 = (bf16[512,256]{1,0:T(8,128)(2,1)S(1)}, bf16[512,256]{1,0:T(8,128)(2,1)S(1)}, u32[]{:S(2)}, u32[]{:S(2)}) collective-permute-start(bf16[512,256]{1,0:T(8,128)(2,1)S(1)} %get-tuple-element.62.refs_7_), channel_id=1, source_target_pairs={{0,2},{1,3},{2,0},{3,1},{4,6},{5,7},{6,4},{7,5},{8,10},{9,11},{10,... | collective-permute-start | bytes 786440 | tf_op jit(solution)/shard_map/ppermute | solution.py:494
  634.6 39.1 %collective-permute-start.22 = (bf16[512,256]{1,0:T(8,128)(2,1)S(1)}, bf16[512,256]{1,0:T(8,128)(2,1)S(1)}, u32[]{:S(2)}, u32[]{:S(2)}) collective-permute-start(bf16[512,256]{1,0:T(8,128)(2,1)S(1)} %get-tuple-element.62.refs_7_), channel_id=1, source_target_pairs={{0,1},{1,0},{2,3},{3,2},{4,5},{5,4},{6,7},{7,6},{8,9},{9,8},{10,11... | collective-permute-start | bytes 786440 | tf_op jit(solution)/shard_map/ppermute | solution.py:494
  634.6 32.9 %collective-permute-start.18 = (bf16[512,256]{1,0:T(8,128)(2,1)S(1)}, bf16[512,256]{1,0:T(8,128)(2,1)S(1)}, u32[]{:S(2)}, u32[]{:S(2)}) collective-permute-start(bf16[512,256]{1,0:T(8,128)(2,1)S(1)} %get-tuple-element.61.refs_6_), channel_id=1, source_target_pairs={{0,2},{1,3},{2,0},{3,1},{4,6},{5,7},{6,4},{7,5},{8,10},{9,11},{10,... | collective-permute-start | bytes 786440 | tf_op jit(solution)/shard_map/ppermute | solution.py:494
  635.1 32.7 %copy-start.10 = (bf16[512,256]{1,0:T(8,128)(2,1)S(1)}, bf16[512,256]{1,0:T(8,128)(2,1)}, u32[]{:S(2)}) copy-start(bf16[512,256]{1,0:T(8,128)(2,1)} %copy-done.9) | copy-start | bytes 786436
  635.1 32.8 %copy-start.8 = (bf16[512,256]{1,0:T(8,128)(2,1)S(1)}, bf16[512,256]{1,0:T(8,128)(2,1)}, u32[]{:S(2)}) copy-start(bf16[512,256]{1,0:T(8,128)(2,1)} %copy-done.7) | copy-start | bytes 786436
  667.5 6.2 collective-permute-start.23
  668.0 6.7 collective-permute-start.20
  671.9 2.7 collective-permute-start.21
  784.5 2.0 copy-start
  825.6 1.9 copy-start.2
Sparse Core Ops, SparseCore 0:
  10.1 83.4 all-gather.3
  95.5 244.5 all-gather.5

commit v2 on v1

--- a/solution.py
+++ b/solution.py
@@ -326,7 +326,7 @@
 def proj(a, w, x):
     n, k = a.shape
     d = w.shape[1]
-    nc = 256
+    nc = 512
     col = pl.BlockSpec((n, nc), lambda i: (0, i))
     return pl.pallas_call(
         proj_kernel, grid=(d // nc,),
@@ -531,12 +531,13 @@
             vs.append(v.reshape(n, kvl, dh))
             n1, w1 = xchg(k, 1), xchg(v, 1)
             n2, w2 = xchg(k, 2), xchg(v, 2)
-            st = attention(bias, q, [(k0, v0), (k1, v1)], (k, v), [], None, False, g)
+            early = [(k0, v0)] if l in full_wo else [(k0, v0), (k1, v1)]
+            st = attention(bias, q, early, (k, v), [], None, False, g)
             k2, v2, n2, w2, st = lax.optimization_barrier((k2, v2, n2, w2, st))
             k3, v3 = far if far is not None else (xchg(k2, 1), xchg(v2, 1))
             n3, w3 = xchg(n2, 1), xchg(w2, 1)
             late = [(jnp.concatenate([n1, n2, n3]), jnp.concatenate([w1, w2, w3]))]
-            last = [(k2, v2), (k3, v3)]
+            last = ([(k1, v1)] if l in full_wo else []) + [(k2, v2), (k3, v3)]
             more = l + 1 < layers
             net = (tp, 2 * l) if l in full_wo else ()
             attn = attention(bias, q, last, None, late, st, True, g, *net)

time: 1010 us -> 997 us (0.987)
  Pallas kernels: 806 us -> 795 us
where the time goes in v2:
time: 997 us; the launch traced here: 990 us
  Pallas kernels  795 us (80%)
  waiting for transfers between devices  132 us (13%)
  local copies, waits for them, and re-layouts  27.8 us (3%)
  between operations  14.6 us (1%)
  starting transfers between devices  11.4 us (1%)
    pallas_call x3, Pallas kernels, matmul_sum(): pl.pallas_call(kern, grid=(steps,), in_specs=[vm, pl.BlockSpec((None, k,...  482 us
    pallas_call x4, Pallas kernels, attention(): pl.pallas_call(kern, grid=(steps,), in_specs=specs, out_specs=out_specs,...  181 us
    all_gather x1, waiting for transfers between devices, whole_wo(): w = lax.all_gather(part, 'tp', axis=0)  84 us
    pallas_call x2, Pallas kernels, gate_up(): pl.pallas_call(gate_kernel, grid=(f // nc,), in_specs=[vm, vm, wspec, wsp...  78.3 us
    ppermute x24, waiting for transfers between devices, xchg(): return lax.ppermute(t, 'sp', [(i, i ^ bit) for i in range(sp)])  48.3 us
    pallas_call x2, Pallas kernels, qkv(): pl.pallas_call(functools.partial(qkv_kernel, nq, dh), grid=(nq + 2,), in_...  31.8 us
    pallas_call x1, Pallas kernels, proj(): pl.pallas_call(proj_kernel, grid=(d // nc,), in_specs=[pl.BlockSpec(memor...  22.8 us
  transfers between devices with their start and end apart: 26, of which 4 were waited for; matrix products, arithmetic and copies ran while one was open for 2% of the time, Pallas kernels for 58%

profile of v2, /device:TPU:0, one launch (start us, length us, event | category | flops | bytes accessed | tf_op | source)
XLA Modules:
  0.0 989.5 jit_solution(8347333337219903683)
XLA Ops:
  7.2 2.3 constant_dynamic-slice_fusion
  9.6 84.0 %all-gather.4.cloned.1.call-done = bf16[4,128,4096]{2,1,0:T(8,128)(2,1)} async-done(((bf16[1,128,4096]{2,1,0:T(8,128)(2,1)}), bf16[4,128,4096]{2,1,0:T(8,128)(2,1)}) %all-gather.4.cloned.1.call-update) | async-done | bytes 4194320 | tf_op jit(solution)/shard_map/all_gather | solution.py:519
  93.6 1.6 copy-done.16
  95.2 1.5 fusion.9
  96.7 1.2 copy.25
  97.8 1.5 collective-permute-start
  99.3 2.2 fusion.8
  101.6 1.1 copy.24
  102.7 0.2 collective-permute-start.5
  102.9 0.6 collective-permute-start.1
  103.5 1.0 fusion
  104.5 0.2 pad_maximum_fusion.6
  104.8 16.9 %qkv.2 = (bf16[512,1024]{1,0:T(8,128)(2,1)S(1)}, bf16[512,256]{1,0:T(8,128)(2,1)S(1)}, bf16[512,256]{1,0:T(8,128)(2,1)S(1)}) custom-call(bf16[512,4096]{1,0:T(8,128)(2,1)} %x_ref.3, bf16[1,4096]{1,0:T(2,128)(2,1)S(1)} %get-tuple-element.84.g_ref, f32[512,128]{1,0:T(8,128)S(1)} %get-tuple-element.88.c_ref, f32[512,128]{1,0:T(8,128)S(1)} %get-tuple-element.89.s_ref, ...), custom_call_target="tpu_custom_call" | custom-call | flops 6442450944 | bytes 8388608 | tf_op jit(solution)/shard_map/qkv/pallas_call | solution.py:68
  121.7 1.0 copy-done.13
  122.7 1.4 collective-permute-start.3
  124.2 0.1 collective-permute-start.10
  124.3 0.7 collective-permute-start.2
  125.0 0.2 copy-done.22
  125.1 0.3 copy-done.23
  125.5 0.6 broadcast_in_dim.18.refs_0_
  126.1 32.2 %attn_first.2 = (f32[512,1024]{1,0:T(8,128)}, f32[512,1024]{1,0:T(8,128)}, f32[512,1024]{1,0:T(8,128)}) custom-call(f32[8,1536]{1,0:T(8,128)} %broadcast_in_dim.18.refs_0_, bf16[512,1024]{1,0:T(8,128)(2,1)} %copy-done.13, bf16[2048,256]{1,0:T(8,128)(2,1)} %bitcast.18.refs_2_, bf16[2048,256]{1,0:T(8,128)(2,1)} %bitcast.17.refs_3_, ...), custom_call_target="tpu_custom_call" | custom-call | flops 19327352832 | bytes 4718592 | tf_op jit(solution)/shard_map/attn_first/pallas_call | solution.py:313
  158.3 43.9 %collective-permute-done.2 = bf16[512,256]{1,0:T(8,128)(2,1)S(1)} collective-permute-done((bf16[512,256]{1,0:T(8,128)(2,1)S(1)}, bf16[512,256]{1,0:T(8,128)(2,1)S(1)}, u32[]{:S(2)}, u32[]{:S(2)}) %collective-permute-start.2) | collective-permute-done | bytes 262176 | tf_op jit(solution)/shard_map/ppermute | solution.py:494
  202.3 0.6 collective-permute-start.11
  202.9 0.1 collective-permute-start.9
  202.9 0.4 collective-permute-start.6
  203.4 0.1 collective-permute-start.7
  203.5 1.7 copy_bitcast_fusion.2
  205.2 1.0 pad_maximum_fusion.1.refs_7_
  206.2 0.9 pad_maximum_fusion.refs_6_
  207.1 1.3 collective-permute-done.6.refs_4_
  208.4 3.0 collective-permute-done.7.refs_5_
  211.4 41.1 %attn_last.2.a_ref = bf16[512,1024]{1,0:T(8,128)(2,1)} custom-call(f32[8,1536]{1,0:T(8,128)} %broadcast_in_dim.18.refs_0_, bf16[512,1024]{1,0:T(8,128)(2,1)} %copy-done.13, bf16[2048,256]{1,0:T(8,128)(2,1)} %collective-permute-done.refs_2_, bf16[2048,256]{1,0:T(8,128)(2,1)} %collective-permute-done.1.refs_3_, ...), custom_call_target="tpu_custom_call" | custom-call | flops 23622320128 | bytes 5767168 | tf_op jit(solution)/shard_map/attn_last/pallas_call | solution.py:313
  252.5 0.1 collective-permute-start.12
  252.6 1.3 collective-permute-start.14
  253.9 0.1 collective-permute-start.13
  254.0 0.8 collective-permute-start.15
  254.8 160.2 %matmul_sum.3.x_ref = bf16[512,4096]{1,0:T(8,128)(2,1)} custom-call(bf16[512,1024]{1,0:T(8,128)(2,1)} %attn_last.2.a_ref, bf16[2,1024,4096]{2,1,0:T(8,128)(2,1)} %w_ref.3, bf16[512,4096]{1,0:T(8,128)(2,1)} %x_ref.3), custom_call_target="tpu_custom_call" | custom-call | flops 99999997952 | bytes 8388608 | tf_op jit(solution)/shard_map/matmul_sum/pallas_call | solution.py:464
  415.1 0.1 collective-permute-start.16
  415.1 0.5 collective-permute-start.17
  415.6 0.4 copy-done.21
  416.0 39.2 %gate_up.2.a_ref = bf16[512,3584]{1,0:T(8,128)(2,1)S(1)} custom-call(bf16[512,4096]{1,0:T(8,128)(2,1)} %matmul_sum.3.x_ref, bf16[1,4096]{1,0:T(2,128)(2,1)S(1)} %get-tuple-element.82.g_ref, bf16[2,4096,3584]{2,1,0:T(8,128)(2,1)} %wg_ref.3, bf16[2,4096,3584]{2,1,0:T(8,128)(2,1)} %wu_ref.3), custom_call_target="tpu_custom_call" | custom-call | flops 30064771072 | bytes 58720256 | tf_op jit(solution)/shard_map/gate_up/pallas_call | solution.py:102
  455.2 1.8 copy-done.1
  457.1 159.3 %matmul_sum.4.x_ref = bf16[512,4096]{1,0:T(8,128)(2,1)} custom-call(bf16[512,3584]{1,0:T(8,128)(2,1)} %copy-done.1, bf16[2,3584,4096]{2,1,0:T(8,128)(2,1)} %w_ref.5, bf16[512,4096]{1,0:T(8,128)(2,1)} %matmul_sum.3.x_ref), custom_call_target="tpu_custom_call" | custom-call | flops 99999997952 | bytes 29360128 | tf_op jit(solution)/shard_map/matmul_sum/pallas_call | solution.py:464
  616.4 14.9 %qkv.3 = (bf16[512,1024]{1,0:T(8,128)(2,1)S(1)}, bf16[512,256]{1,0:T(8,128)(2,1)S(1)}, bf16[512,256]{1,0:T(8,128)(2,1)S(1)}) custom-call(bf16[512,4096]{1,0:T(8,128)(2,1)} %matmul_sum.4.x_ref, bf16[1,4096]{1,0:T(2,128)(2,1)S(1)} %get-tuple-element.83.g_ref, f32[512,128]{1,0:T(8,128)S(1)} %copy-done.4, f32[512,128]{1,0:T(8,128)S(1)} %copy-done.6, ...), custom_call_target="tpu_custom_call" | custom-call | flops 6442450944 | bytes 8388608 | tf_op jit(solution)/shard_map/qkv/pallas_call | solution.py:68
  631.4 1.0 copy-done.14
  632.4 1.5 collective-permute-start.19
  633.9 0.5 collective-permute-start.18
  634.4 20.0 %attn_first.3 = (f32[512,1024]{1,0:T(8,128)}, f32[512,1024]{1,0:T(8,128)}, f32[512,1024]{1,0:T(8,128)}) custom-call(f32[8,1536]{1,0:T(8,128)} %broadcast_in_dim.18.refs_0_, bf16[512,1024]{1,0:T(8,128)(2,1)} %copy-done.14, bf16[2048,256]{1,0:T(8,128)(2,1)} %get-tuple-element.53.refs_2_, bf16[2048,256]{1,0:T(8,128)(2,1)} %get-tuple-element.54.refs_3_, ...), custom_call_target="tpu_custom_call" | custom-call | flops 10737418240 | bytes 2621440 | tf_op jit(solution)/shard_map/attn_first/pallas_call | solution.py:313
  654.5 0.3 collective-permute-start.23
  654.9 0.3 collective-permute-start.20
  655.3 1.0 stack_reshape.13
  656.3 1.0 stack_reshape.15
  657.3 1.6 pad_maximum_fusion.4
  658.9 0.2 collective-permute-start.21
  659.1 1.6 pad_maximum_fusion.5
  660.7 0.9 pad_maximum_fusion.3.refs_9_
  661.6 1.0 pad_maximum_fusion.2.refs_8_
  662.6 87.2 %attn_last.3.a_ref = bf16[512,4096]{1,0:T(8,128)(2,1)} custom-call(f32[8,1536]{1,0:T(8,128)} %broadcast_in_dim.18.refs_0_, bf16[512,1024]{1,0:T(8,128)(2,1)} %copy-done.14, bf16[2048,256]{1,0:T(8,128)(2,1)} %copy-done.21, bf16[2048,256]{1,0:T(8,128)(2,1)} %collective-permute-done.13.refs_3_, bf16[2048,256]{1,0:T(8,128)(2,1)} %collective-permute-done.14.refs_4_, ...), custom_call_target="tpu_custom_call" | custom-call | flops 32212254720 | bytes 7864320 | tf_op jit(solution)/shard_map/attn_last/pallas_call | solution.py:313
  749.8 22.8 %proj.1.x_ref = bf16[512,4096]{1,0:T(8,128)(2,1)S(1)} custom-call(bf16[512,4096]{1,0:T(8,128)(2,1)} %attn_last.3.a_ref, bf16[4096,4096]{1,0:T(8,128)(2,1)} %bitcast.23, bf16[512,4096]{1,0:T(8,128)(2,1)} %matmul_sum.4.x_ref), custom_call_target="tpu_custom_call" | custom-call | flops 17179869184 | bytes 33554432 | tf_op jit(solution)/shard_map/proj/pallas_call | solution.py:331
  772.6 2.0 copy-done
  774.6 39.1 %gate_up.3.a_ref = bf16[512,3584]{1,0:T(8,128)(2,1)S(1)} custom-call(bf16[512,4096]{1,0:T(8,128)(2,1)} %copy-done, bf16[1,4096]{1,0:T(2,128)(2,1)S(1)} %get-tuple-element.81.g_ref, bf16[2,4096,3584]{2,1,0:T(8,128)(2,1)} %wg_ref.3, bf16[2,4096,3584]{2,1,0:T(8,128)(2,1)} %wu_ref.3), custom_call_target="tpu_custom_call" | custom-call | flops 30064771072 | bytes 58720256 | tf_op jit(solution)/shard_map/gate_up/pallas_call | solution.py:102
  813.8 1.8 copy-done.2
  815.6 162.2 %matmul_sum.5 = bf16[512,4096]{1,0:T(8,128)(2,1)} custom-call(bf16[512,3584]{1,0:T(8,128)(2,1)} %copy-done.2, bf16[2,3584,4096]{2,1,0:T(8,128)(2,1)} %w_ref.5, bf16[512,4096]{1,0:T(8,128)(2,1)} %copy-done), custom_call_target="tpu_custom_call" | custom-call | flops 99999997952 | bytes 29360128 | tf_op jit(solution)/shard_map/matmul_sum/pallas_call | solution.py:464
  977.8 4.7 copy.27
  (75 shorter events, 0.5 us)
Async XLA Ops:
  7.2 86.4 %all-gather.4.cloned.1.call-start = ((), (), s32[]{:S(2)}) async-start(), calls=%async_computation | async-start | bytes 5242880 | tf_op jit(solution)/shard_map/all_gather | solution.py:519
  9.5 740.2 %all-gather.6.cloned.1.call-start = ((), (), s32[]{:S(2)}) async-start(), calls=%async_computation.1 | async-start | bytes 37748736 | tf_op jit(solution)/shard_map/all_gather | solution.py:520
  93.6 1.6 copy-start.16
  96.7 2.6 copy-start.17
  97.8 26.3 %collective-permute-start.4 = (bf16[2048,256]{1,0:T(8,128)(2,1)}, bf16[2048,256]{1,0:T(8,128)(2,1)S(1)}, u32[]{:S(2)}, u32[]{:S(2)}) collective-permute-start(bf16[2048,256]{1,0:T(8,128)(2,1)} %bitcast.18.refs_2_), channel_id=1, source_target_pairs={{0,1},{1,0},{2,3},{3,2},{4,5},{5,4},{6,7},{7,6},{8,9},{9,8},{10,11... | collective-permute-start | bytes 3145736 | tf_op jit(solution)/shard_map/ppermute | solution.py:494
  97.8 104.4 %collective-permute-start = (bf16[2048,256]{1,0:T(8,128)(2,1)}, bf16[2048,256]{1,0:T(8,128)(2,1)}, u32[]{:S(2)}, u32[]{:S(2)}) collective-permute-start(bf16[2048,256]{1,0:T(8,128)(2,1)} %bitcast.18.refs_2_), channel_id=1, source_target_pairs={{0,2},{1,3},{2,0},{3,1},{4,6},{5,7},{6,4},{7,5},{8,10},{9,11},{10,... | collective-permute-start | bytes 3145736 | tf_op jit(solution)/shard_map/ppermute | solution.py:494
  101.6 1.9 copy-start.20
  101.6 3.2 copy-start.18
  102.7 21.5 %collective-permute-start.5 = (bf16[2048,256]{1,0:T(8,128)(2,1)}, bf16[2048,256]{1,0:T(8,128)(2,1)S(1)}, u32[]{:S(2)}, u32[]{:S(2)}) collective-permute-start(bf16[2048,256]{1,0:T(8,128)(2,1)} %bitcast.17.refs_3_), channel_id=1, source_target_pairs={{0,1},{1,0},{2,3},{3,2},{4,5},{5,4},{6,7},{7,6},{8,9},{9,8},{10,11... | collective-permute-start | bytes 3145736 | tf_op jit(solution)/shard_map/ppermute | solution.py:494
  102.9 99.4 %collective-permute-start.1 = (bf16[2048,256]{1,0:T(8,128)(2,1)}, bf16[2048,256]{1,0:T(8,128)(2,1)}, u32[]{:S(2)}, u32[]{:S(2)}) collective-permute-start(bf16[2048,256]{1,0:T(8,128)(2,1)} %bitcast.17.refs_3_), channel_id=1, source_target_pairs={{0,2},{1,3},{2,0},{3,1},{4,6},{5,7},{6,4},{7,5},{8,10},{9,11},{10,... | collective-permute-start | bytes 3145736 | tf_op jit(solution)/shard_map/ppermute | solution.py:494
  104.8 17.0 %copy-start.3 = (f32[512,128]{1,0:T(8,128)}, f32[512,128]{1,0:T(8,128)S(1)}, u32[]{:S(2)}) copy-start(f32[512,128]{1,0:T(8,128)S(1)} %get-tuple-element.88.c_ref) | copy-start | bytes 786436
  104.8 17.0 %copy-start.5 = (f32[512,128]{1,0:T(8,128)}, f32[512,128]{1,0:T(8,128)S(1)}, u32[]{:S(2)}) copy-start(f32[512,128]{1,0:T(8,128)S(1)} %get-tuple-element.89.s_ref) | copy-start | bytes 786436
  104.8 19.3 %copy-start.19 = (bf16[2,4096]{1,0:T(2,128)(2,1)S(1)}, bf16[2,4096]{1,0:T(2,128)(2,1)}, u32[]{:S(2)}) copy-start(bf16[2,4096]{1,0:T(2,128)(2,1)} %param.25) | copy-start | bytes 49156
  121.7 1.0 copy-start.13
  122.7 3.4 copy-start.7
  122.7 3.4 copy-start.9
  122.7 79.6 %collective-permute-start.3 = (bf16[512,256]{1,0:T(8,128)(2,1)S(1)}, bf16[512,256]{1,0:T(8,128)(2,1)S(1)}, u32[]{:S(2)}, u32[]{:S(2)}) collective-permute-start(bf16[512,256]{1,0:T(8,128)(2,1)S(1)} %get-tuple-element.42.refs_7_), channel_id=1, source_target_pairs={{0,2},{1,3},{2,0},{3,1},{4,6},{5,7},{6,4},{7,5},{8,10},{9,11},{10,... | collective-permute-start | bytes 786440 | tf_op jit(solution)/shard_map/ppermute | solution.py:494
  124.1 1.0 copy-start.22
  124.2 79.2 %collective-permute-start.10 = (bf16[512,256]{1,0:T(8,128)(2,1)S(1)}, bf16[512,256]{1,0:T(8,128)(2,1)S(1)}, u32[]{:S(2)}, u32[]{:S(2)}) collective-permute-start(bf16[512,256]{1,0:T(8,128)(2,1)S(1)} %get-tuple-element.42.refs_7_), channel_id=1, source_target_pairs={{0,1},{1,0},{2,3},{3,2},{4,5},{5,4},{6,7},{7,6},{8,9},{9,8},{10,11... | collective-permute-start | bytes 786440 | tf_op jit(solution)/shard_map/ppermute | solution.py:494
  124.2 1.2 copy-start.23
  124.3 78.0 %collective-permute-start.2 = (bf16[512,256]{1,0:T(8,128)(2,1)S(1)}, bf16[512,256]{1,0:T(8,128)(2,1)S(1)}, u32[]{:S(2)}, u32[]{:S(2)}) collective-permute-start(bf16[512,256]{1,0:T(8,128)(2,1)S(1)} %get-tuple-element.41.refs_6_), channel_id=1, source_target_pairs={{0,2},{1,3},{2,0},{3,1},{4,6},{5,7},{6,4},{7,5},{8,10},{9,11},{10,... | collective-permute-start | bytes 786440 | tf_op jit(solution)/shard_map/ppermute | solution.py:494
  126.1 77.4 %copy-start.15 = (bf16[1,2048,2,128]{3,2,1,0:T(2,128)(2,1)S(1)}, bf16[1,2048,2,128]{3,2,1,0:T(2,128)(2,1)}, u32[]{:S(2)}) copy-start(bf16[1,2048,2,128]{3,2,1,0:T(2,128)(2,1)} %get-tuple-element.78) | copy-start | bytes 3145732
  202.3 3.9 collective-permute-start.8
  202.3 2.9 collective-permute-start.11
  202.9 3.3 collective-permute-start.9
  202.9 5.4 collective-permute-start.6
  203.4 8.0 collective-permute-start.7
  252.5 162.5 %collective-permute-start.12 = (bf16[2048,256]{1,0:T(8,128)(2,1)}, bf16[2048,256]{1,0:T(8,128)(2,1)S(1)}, u32[]{:S(2)}, u32[]{:S(2)}) collective-permute-start(bf16[2048,256]{1,0:T(8,128)(2,1)} %get-tuple-element.53.refs_2_), channel_id=1, source_target_pairs={{0,1},{1,0},{2,3},{3,2},{4,5},{5,4},{6,7},{7,6},{8,9},{9,8},{10,11... | collective-permute-start | bytes 3145736 | tf_op jit(solution)/shard_map/ppermute | solution.py:494
  252.6 162.4 %collective-permute-start.14 = (bf16[2048,256]{1,0:T(8,128)(2,1)}, bf16[2048,256]{1,0:T(8,128)(2,1)}, u32[]{:S(2)}, u32[]{:S(2)}) collective-permute-start(bf16[2048,256]{1,0:T(8,128)(2,1)} %get-tuple-element.53.refs_2_), channel_id=1, source_target_pairs={{0,2},{1,3},{2,0},{3,1},{4,6},{5,7},{6,4},{7,5},{8,10},{9,11},{10,... | collective-permute-start | bytes 3145736 | tf_op jit(solution)/shard_map/ppermute | solution.py:494
  253.9 161.1 %collective-permute-start.13 = (bf16[2048,256]{1,0:T(8,128)(2,1)}, bf16[2048,256]{1,0:T(8,128)(2,1)}, u32[]{:S(2)}, u32[]{:S(2)}) collective-permute-start(bf16[2048,256]{1,0:T(8,128)(2,1)} %get-tuple-element.54.refs_3_), channel_id=1, source_target_pairs={{0,1},{1,0},{2,3},{3,2},{4,5},{5,4},{6,7},{7,6},{8,9},{9,8},{10,11... | collective-permute-start | bytes 3145736 | tf_op jit(solution)/shard_map/ppermute | solution.py:494
  254.0 161.0 %collective-permute-start.15 = (bf16[2048,256]{1,0:T(8,128)(2,1)}, bf16[2048,256]{1,0:T(8,128)(2,1)}, u32[]{:S(2)}, u32[]{:S(2)}) collective-permute-start(bf16[2048,256]{1,0:T(8,128)(2,1)} %get-tuple-element.54.refs_3_), channel_id=1, source_target_pairs={{0,2},{1,3},{2,0},{3,1},{4,6},{5,7},{6,4},{7,5},{8,10},{9,11},{10,... | collective-permute-start | bytes 3145736 | tf_op jit(solution)/shard_map/ppermute | solution.py:494
  415.0 1.0 copy-start.21
  415.1 42.0 %collective-permute-start.16 = (bf16[2048,256]{1,0:T(8,128)(2,1)}, bf16[2048,256]{1,0:T(8,128)(2,1)}, u32[]{:S(2)}, u32[]{:S(2)}) collective-permute-start(bf16[2048,256]{1,0:T(8,128)(2,1)} %collective-permute-done.14.refs_4_), channel_id=1, source_target_pairs={{0,1},{1,0},{2,3},{3,2},{4,5},{5,4},{6,7},{7,6},{8,9},{9,8},{10,11... | collective-permute-start | bytes 3145736 | tf_op jit(solution)/shard_map/ppermute | solution.py:494
  415.1 41.9 %collective-permute-start.17 = (bf16[2048,256]{1,0:T(8,128)(2,1)}, bf16[2048,256]{1,0:T(8,128)(2,1)}, u32[]{:S(2)}, u32[]{:S(2)}) collective-permute-start(bf16[2048,256]{1,0:T(8,128)(2,1)} %collective-permute-done.15.refs_5_), channel_id=1, source_target_pairs={{0,1},{1,0},{2,3},{3,2},{4,5},{5,4},{6,7},{7,6},{8,9},{9,8},{10,11... | collective-permute-start | bytes 3145736 | tf_op jit(solution)/shard_map/ppermute | solution.py:494
  455.2 1.8 copy-start.1
  457.1 159.4 %copy-start.4 = (f32[512,128]{1,0:T(8,128)S(1)}, f32[512,128]{1,0:T(8,128)}, u32[]{:S(2)}) copy-start(f32[512,128]{1,0:T(8,128)} %copy-done.3) | copy-start | bytes 786436
  457.1 159.4 %copy-start.6 = (f32[512,128]{1,0:T(8,128)S(1)}, f32[512,128]{1,0:T(8,128)}, u32[]{:S(2)}) copy-start(f32[512,128]{1,0:T(8,128)} %copy-done.5) | copy-start | bytes 786436
  631.3 1.0 copy-start.14
  632.4 2.0 copy-start.11
  632.4 2.0 copy-start.12
  632.4 22.1 %collective-permute-start.19 = (bf16[512,256]{1,0:T(8,128)(2,1)S(1)}, bf16[512,256]{1,0:T(8,128)(2,1)S(1)}, u32[]{:S(2)}, u32[]{:S(2)}) collective-permute-start(bf16[512,256]{1,0:T(8,128)(2,1)S(1)} %get-tuple-element.64.refs_5_), channel_id=1, source_target_pairs={{0,2},{1,3},{2,0},{3,1},{4,6},{5,7},{6,4},{7,5},{8,10},{9,11},{10,... | collective-permute-start | bytes 786440 | tf_op jit(solution)/shard_map/ppermute | solution.py:494
  633.9 26.8 %collective-permute-start.22 = (bf16[512,256]{1,0:T(8,128)(2,1)S(1)}, bf16[512,256]{1,0:T(8,128)(2,1)S(1)}, u32[]{:S(2)}, u32[]{:S(2)}) collective-permute-start(bf16[512,256]{1,0:T(8,128)(2,1)S(1)} %get-tuple-element.64.refs_5_), channel_id=1, source_target_pairs={{0,1},{1,0},{2,3},{3,2},{4,5},{5,4},{6,7},{7,6},{8,9},{9,8},{10,11... | collective-permute-start | bytes 786440 | tf_op jit(solution)/shard_map/ppermute | solution.py:494
  633.9 20.6 %collective-permute-start.18 = (bf16[512,256]{1,0:T(8,128)(2,1)S(1)}, bf16[512,256]{1,0:T(8,128)(2,1)S(1)}, u32[]{:S(2)}, u32[]{:S(2)}) collective-permute-start(bf16[512,256]{1,0:T(8,128)(2,1)S(1)} %get-tuple-element.63.refs_4_), channel_id=1, source_target_pairs={{0,2},{1,3},{2,0},{3,1},{4,6},{5,7},{6,4},{7,5},{8,10},{9,11},{10,... | collective-permute-start | bytes 786440 | tf_op jit(solution)/shard_map/ppermute | solution.py:494
  634.4 20.4 %copy-start.10 = (bf16[512,256]{1,0:T(8,128)(2,1)S(1)}, bf16[512,256]{1,0:T(8,128)(2,1)}, u32[]{:S(2)}) copy-start(bf16[512,256]{1,0:T(8,128)(2,1)} %copy-done.9) | copy-start | bytes 786436
  634.4 20.4 %copy-start.8 = (bf16[512,256]{1,0:T(8,128)(2,1)S(1)}, bf16[512,256]{1,0:T(8,128)(2,1)}, u32[]{:S(2)}) copy-start(bf16[512,256]{1,0:T(8,128)(2,1)} %copy-done.7) | copy-start | bytes 786436
  654.5 6.2 collective-permute-start.23
  654.9 6.7 collective-permute-start.20
  658.9 2.7 collective-permute-start.21
  772.6 2.0 copy-start
  813.8 1.9 copy-start.2
Sparse Core Ops, SparseCore 0:
  10.1 83.4 all-gather.3
  95.5 244.4 all-gather.5
